TPU v7x, 32 devices: a whole 2x2x4 slice. The times are simulated.
32 devices in a mesh: rows: 8 (over y, x, core), model: 4 (over z).
Axes of the slice: x: 2, y: 2, z: 4, core: 2. Of those that a mesh axis runs over, the one named last changes fastest.
Arguments:
- weight_gate: bfloat16 [2048, 8192], P('rows', 'model'), may hold values from -0.125 to 0.125
- low_gate: bfloat16 [2048, 64], P('rows'), may hold values from -0.125 to 0.125
- high_gate: bfloat16 [64, 8192], P(None, 'model'), may hold values from -0.75 to 0.75
- weight_up: bfloat16 [2048, 8192], P('rows', 'model'), may hold values from -0.125 to 0.125
- low_up: bfloat16 [2048, 64], P('rows'), may hold values from -0.125 to 0.125
- high_up: bfloat16 [64, 8192], P(None, 'model'), may hold values from -0.75 to 0.75
- weight_down: bfloat16 [8192, 2048], P('model', 'rows'), may hold values from -0.0625 to 0.0625
- low_down: bfloat16 [8192, 64], P('model'), may hold values from -0.0625 to 0.0625
- high_down: bfloat16 [64, 2048], P(None, 'rows'), may hold values from -0.75 to 0.75
- norm_train: float32 [2048], P(('rows', 'model')), may hold values from 0.25 to 1.75
- norm_step: float32 [2048], P(('rows', 'model')), may hold values from -0.3 to 0.3
Outputs:
- final_gate: bfloat16 [8192, 2048], P('model')
- final_up: bfloat16 [8192, 2048], P('model')
- final_down: bfloat16 [2048, 8192], P(None, 'model')
- serve_norm: bfloat16 [2048], replicated
All inputs are finite; a program needn't handle non-finite values.
Results may differ from a plain program's by a relative error of at most 0.001.
Values may be sent and summed in bfloat16 or wider, within the bound.
A program may use at most 192 MiB of HBM per device.

v0:
```python
import functools

import jax
import jax.numpy as jnp
from jax import lax
from jax.experimental import pallas as pl
from jax.experimental.pallas import tpu as pltpu
from jax.sharding import PartitionSpec as P

mix_rate = 0.5
MESH = pl.DeviceIdType.MESH
PIECES = 4
STRIPS = 1
SIDE = 2


def gather_kernel(
    rows,
    model,
    *refs,
):
    sources, (og, ou, od, norm), refs = refs[:11], refs[11:15], refs[15:]
    held, refs = refs[:11], refs[11:]
    wg, lg, hg, wu, lu, hu, wd, ld, hd, nt, ns = held
    fetch_sem, link_send, link_recv, pair_send, pair_recv, norm_send, norm_recv = refs
    me = lax.axis_index("rows")
    depth = lax.axis_index("model")
    core = lax.rem(me, 2)
    x = lax.rem(me // 2, SIDE)
    y = me // (2 * SIDE)

    def device(y, x, core):
        return (y * SIDE + x) * 2 + core

    pair = device(y, x, 1 - core)
    near_x = device(y, 1 - x, core)
    near_y = device(1 - y, x, core)
    far = device(1 - y, 1 - x, core)

    def shifted(position, size, step):
        return lax.rem(position + step, size)

    barrier = pltpu.get_barrier_semaphore()
    for step in range(1, rows):
        pl.semaphore_signal(barrier, inc=1, device_id={"rows": shifted(me, rows, step)}, device_id_type=MESH)
    for step in range(1, model):
        pl.semaphore_signal(barrier, inc=1, device_id={"model": shifted(depth, model, step)}, device_id_type=MESH)

    outs = (og, ou, od)
    fetches = {}

    def fetch(key, i, *cut):
        fetches[key] = pltpu.make_async_copy(
            sources[i].at[cut] if cut else sources[i], held[i].at[cut] if cut else held[i],
            fetch_sem.at[len(fetches)],
        )

    long = wg.shape[1] // PIECES
    long_down = wd.shape[0] // PIECES
    short = wg.shape[0]
    short_down = wd.shape[1]
    units = [(a, k) for k in range(PIECES) for a in range(3)]

    for u, (a, k) in enumerate(units):
        if k == 0:
            fetch(("low", a), 3 * a + 1)
            fetch(("high", a), 3 * a + 2)
        if a < 2:
            fetch(u, 3 * a, pl.ds(0, short), pl.ds(k * long, long))
        else:
            fetch(u, 3 * a, pl.ds(k * long_down, long_down), pl.ds(0, short_down))
    fetch("train", 9)
    fetch("step", 10)
    for f in fetches.values():
        f.start()

    def place(u, owner):
        a, k = units[u]
        if a < 2:
            return outs[a].at[pl.ds(k * long, long), pl.ds(pl.multiple_of(owner * short, short), short)]
        return outs[a].at[pl.ds(pl.multiple_of(owner * short_down, short_down), short_down), pl.ds(k * long_down, long_down)]

    def compute(u):
        a, k = units[u]
        if k == 0:
            fetches["low", a].wait()
            fetches["high", a].wait()
        fetches[u].wait()
        if a < 2:
            w, low, high = ((wg, lg, hg), (wu, lu, hu))[a]
            cut = slice(k * long, (k + 1) * long)
            weight, low, high = w[:, cut], low[...], high[:, cut]
        else:
            cut = slice(k * long_down, (k + 1) * long_down)
            weight, low, high = wd[cut, :], ld[:, cut], hd[...]
        merged = weight.astype(jnp.float32) + mix_rate * lax.dot_general(
            low, high, (((0,), (0,)), ((), ())), preferred_element_type=jnp.float32
        )
        place(u, me)[...] = merged.astype(jnp.bfloat16).T

    def copy(u, owner, send, recv, target):
        return pltpu.make_async_remote_copy(
            src_ref=place(u, owner), dst_ref=place(u, owner), send_sem=send, recv_sem=recv,
            device_id={"rows": target}, device_id_type=MESH,
        )

    def link(lane, u, owner, target):
        return copy(u, owner, link_send.at[lane, u], link_recv.at[lane, u], target)

    def across(lane, u, owner):
        return copy(u, owner, pair_send.at[lane, u], pair_recv.at[lane, u], pair)

    def send_own(u):
        link(0, u, me, near_x).start()
        link(1, u, me, near_y).start()
        across(3, u, me).start()

    count = len(units)
    compute(0)
    fetches["train"].wait()
    fetches["step"].wait()
    norm[me, depth] = jnp.zeros(norm.shape[2:], norm.dtype)
    norm[me, depth, :, : nt.shape[1]] = nt[...] + ns[...]
    pl.semaphore_wait(barrier, rows - 1 + model - 1)
    for u in range(1, count):
        compute(u)
        send_own(u - 1)

    def norm_copy(step, send):
        if step < model:
            to = {"model": shifted(depth, model, step)}
            ref = norm.at[me, depth] if send else norm.at[me, shifted(depth, model, model - step)]
            slot = step - 1
        else:
            step = step - model + 1
            to = {"rows": shifted(me, rows, step)}
            ref = norm.at[me] if send else norm.at[shifted(me, rows, rows - step)]
            slot = model - 1 + step - 1
        return pltpu.make_async_remote_copy(
            src_ref=ref, dst_ref=ref, send_sem=norm_send.at[slot], recv_sem=norm_recv.at[slot],
            device_id=to, device_id_type=MESH,
        )

    for step in range(1, model):
        norm_copy(step, True).start()
    send_own(count - 1)
    for step in range(1, model):
        norm_copy(step, False).wait_recv()
    for step in range(model, model + rows - 1):
        norm_copy(step, True).start()

    for u in range(count):
        link(0, u, near_x, near_x).wait_recv()
        if u % 2 == 0:
            link(2, u, near_x, near_y).start()
        across(0, u, near_x).start()
        link(1, u, near_y, near_y).wait_recv()
        if u % 2 == 1:
            link(2, u, near_y, near_x).start()
        across(1, u, near_y).start()
    for u in range(count):
        link(2, u, far, near_x).wait_recv()
        across(2, u, far).start()

    for step in range(model, model + rows - 1):
        norm_copy(step, False).wait_recv()
    for step in range(1, model + rows - 1):
        norm_copy(step, True).wait_send()
    pair_x, pair_y = device(y, 1 - x, 1 - core), device(1 - y, x, 1 - core)
    pair_far = device(1 - y, 1 - x, 1 - core)
    for u in range(count):
        link(0, u, me, near_x).wait_send()
        link(1, u, me, near_y).wait_send()
        link(2, u, near_x if u % 2 == 0 else near_y, near_x).wait_send()
        for lane, mine, theirs in ((3, me, pair), (0, near_x, pair_x), (1, near_y, pair_y), (2, far, pair_far)):
            across(lane, u, mine).wait_send()
            across(lane, u, theirs).wait_recv()


def gathered(rows, model, arrays):
    weight_gate, weight_up, weight_down, norm_train = arrays[0], arrays[3], arrays[6], arrays[9]
    shapes = [
        (weight_gate.shape[1], weight_gate.shape[0] * rows),
        (weight_up.shape[1], weight_up.shape[0] * rows),
        (weight_down.shape[1] * rows, weight_down.shape[0]),
    ]
    lanes = -(-norm_train.shape[1] // 128) * 128
    count = 3 * PIECES
    small = rows - 1 + model - 1
    dma = pltpu.SemaphoreType.DMA
    vmem = pl.BlockSpec(memory_space=pltpu.VMEM)
    return pl.pallas_call(
        functools.partial(gather_kernel, rows, model),
        out_shape=[pltpu.VMEM(s, jnp.bfloat16) for s in shapes] + [pltpu.VMEM((rows, model, 1, lanes), jnp.float32)],
        in_specs=[pl.BlockSpec(memory_space=pltpu.HBM)] * len(arrays),
        out_specs=[vmem] * 4,
        scratch_shapes=[pltpu.VMEM(a.shape, a.dtype) for a in arrays]
        + [
            dma((count + 8,)),
            dma((3, count)), dma((3, count)), dma((4, count)), dma((4, count)), dma((small,)), dma((small,)),
        ],
        compiler_params=pltpu.CompilerParams(collective_id=0, has_side_effects=True, vmem_limit_bytes=39 * 2**20 + 5 * 2**17),
    )(*arrays)


def write_kernel(size, lanes, g, u, d, norm, og, ou, od, out, sems):
    strip = g.shape[0] // STRIPS
    copies = [
        pltpu.make_async_copy(s.at[pl.ds(k * strip, strip)], t.at[pl.ds(k * strip, strip)], sems.at[i, k])
        for k in range(STRIPS)
        for i, (s, t) in enumerate(((g, og), (u, ou), (d, od)))
    ]
    for c in copies:
        c.start()
    rows, model = norm.shape[:2]
    parts = [norm[r, m][:, :size] for r in range(rows) for m in range(model)]
    group = lanes // size
    packed = [jnp.concatenate(parts[i : i + group], axis=1) for i in range(0, len(parts), group)]
    out[...] = jnp.concatenate(packed, axis=0).astype(out.dtype)
    for c in copies:
        c.wait()


def written(size, arrays):
    lanes = arrays[3].shape[3]
    total = arrays[3].shape[0] * arrays[3].shape[1] * size
    hbm, vmem = pl.BlockSpec(memory_space=pltpu.HBM), pl.BlockSpec(memory_space=pltpu.VMEM)
    return pl.pallas_call(
        functools.partial(write_kernel, size, lanes),
        out_shape=[jax.ShapeDtypeStruct(a.shape, a.dtype) for a in arrays[:3]]
        + [jax.ShapeDtypeStruct((total // lanes, lanes), jnp.bfloat16)],
        in_specs=[vmem] * 4,
        out_specs=[hbm] * 3 + [vmem],
        scratch_shapes=[pltpu.SemaphoreType.DMA((3, STRIPS))],
        compiler_params=pltpu.CompilerParams(vmem_limit_bytes=2**20),
    )(*arrays)


def local_kernel(rows, model, *arrays):
    arrays = tuple(a.T if i in (1, 4, 7) else a for i, a in enumerate(arrays[:9])) + tuple(
        a.reshape(1, -1) for a in arrays[9:]
    )
    gate, up, down, norm = gathered(rows, model, arrays)
    gate, up, down, serve_norm = written(arrays[9].shape[1], (gate, up, down, norm))
    return gate, up, down, serve_norm.reshape(-1)


def merge(weight, low, high):
    full = weight.astype(jnp.float32) + mix_rate * jnp.dot(low, high, preferred_element_type=jnp.float32)
    return full.astype(jnp.bfloat16).T


def local_plain(*arrays):
    gate, up, down = merge(*arrays[:3]), merge(*arrays[3:6]), merge(*arrays[6:9])
    return (
        lax.all_gather(gate, "rows", axis=1, tiled=True),
        lax.all_gather(up, "rows", axis=1, tiled=True),
        lax.all_gather(down, "rows", axis=0, tiled=True),
        lax.all_gather((arrays[9] + arrays[10]).astype(jnp.bfloat16), ("rows", "model"), axis=0, tiled=True),
    )


def solution(mesh):
    rows, model = mesh.shape["rows"], mesh.shape["model"]
    local = functools.partial(local_kernel, rows, model) if rows == 2 * SIDE * SIDE else local_plain
    in_specs = (
        P("rows", "model"), P("rows", None), P(None, "model"),
        P("rows", "model"), P("rows", None), P(None, "model"),
        P("model", "rows"), P("model", None), P(None, "rows"),
        P(("rows", "model")), P(("rows", "model")),
    )
    out_specs = (P("model", None), P("model", None), P(None, "model"), P())
    return jax.shard_map(local, mesh=mesh, in_specs=in_specs, out_specs=out_specs, check_vma=False)
```

profile of v0, /device:TPU:0, one launch (start us, length us, event | category | flops | bytes accessed | tf_op | source)
XLA Modules:
  0.0 122.1 jit_solution(7022164548023786989)
XLA Ops:
  0.6 112.1 %shard_map.138 = (bf16[2048,2048]{1,0:T(8,128)(2,1)S(1)}, bf16[2048,2048]{1,0:T(8,128)(2,1)S(1)}, bf16[2048,2048]{1,0:T(8,128)(2,1)S(1)}, f32[8,4,1,128]{3,2,1,0:T(1,128)S(1)}) custom-call(bf16[256,2048]{1,0:T(8,128)(2,1)} %refs_0_.1, bf16[64,256]{1,0:T(8,128)(2,1)} %bitcast.7, bf16[64,2048]{1,0:T(8,128)(2,1)} %refs_2_.1, bf16[256,2048]{1,0:T(8,128)(2,1)} %refs_3_.1, ...), custom_call_target="tpu_custom_call" | custom-call | tf_op jit(solution)/shard_map/pallas_call | solution.py:192
  112.8 9.3 %shard_map.139 = (bf16[2048,2048]{1,0:T(8,128)(2,1)}, bf16[2048,2048]{1,0:T(8,128)(2,1)}, bf16[2048,2048]{1,0:T(8,128)(2,1)}, bf16[16,128]{1,0:T(8,128)(2,1)}) custom-call(bf16[2048,2048]{1,0:T(8,128)(2,1)S(1)} %get-tuple-element.12.g, bf16[2048,2048]{1,0:T(8,128)(2,1)S(1)} %get-tuple-element.13.u, bf16[2048,2048]{1,0:T(8,128)(2,1)S(1)} %get-tuple-element.14.d, ...), custom_call_target="tpu_custom_call" | custom-call | tf_op jit(solution)/shard_map/pallas_call | solution.py:228
where the time goes:
time: 122 us
  Pallas kernels  121 us (99%)
    pallas_call x1, Pallas kernels, gathered(): pl.pallas_call(functools.partial(gather_kernel, rows, model), out_shape=[...  112 us
    pallas_call x1, Pallas kernels, written(): pl.pallas_call(functools.partial(write_kernel, size, lanes), out_shape=[j...  9.3 us

commit v1 on v0

v1 whole, which is shorter than its diff:
```python
import functools

import jax
import jax.numpy as jnp
from jax import lax
from jax.experimental import pallas as pl
from jax.experimental.pallas import tpu as pltpu
from jax.sharding import PartitionSpec as P

mix_rate = 0.5
MESH = pl.DeviceIdType.MESH
PIECES = 4
STRIPS = 1
DOWN_PIECES = 8
EARLY = 6
SIDE = 2


class Place:
    def __init__(self):
        self.me = me = lax.axis_index("rows")
        self.core = core = lax.rem(me, 2)
        x = lax.rem(me // 2, SIDE)
        y = me // (2 * SIDE)

        def device(y, x, core):
            return (y * SIDE + x) * 2 + core

        self.near_x, self.near_y = device(y, 1 - x, core), device(1 - y, x, core)
        self.far = device(1 - y, 1 - x, core)
        self.pair = device(y, x, 1 - core)
        self.pair_x, self.pair_y = device(y, 1 - x, 1 - core), device(1 - y, x, 1 - core)
        self.pair_far = device(1 - y, 1 - x, 1 - core)


def remote(src, dst, send, recv, target):
    return pltpu.make_async_remote_copy(
        src_ref=src, dst_ref=dst, send_sem=send, recv_sem=recv, device_id={"rows": target}, device_id_type=MESH
    )


def shifted(position, size, step):
    return lax.rem(position + step, size)


def first_kernel(rows, model, *refs):
    sources, (og, ou, own, early, norm), refs = refs[:11], refs[11:16], refs[16:]
    held, refs = refs[:11], refs[11:]
    wg, lg, hg, wu, lu, hu, wd, ld, hd, nt, ns = held
    fetch_sem, link_send, link_recv, pair_send, pair_recv, early_send, early_recv, norm_send, norm_recv = refs
    at = Place()
    me, near_x, near_y, far, pair = at.me, at.near_x, at.near_y, at.far, at.pair
    depth = lax.axis_index("model")

    barrier = pltpu.get_barrier_semaphore()
    for step in range(1, rows):
        pl.semaphore_signal(barrier, inc=1, device_id={"rows": shifted(me, rows, step)}, device_id_type=MESH)
    for step in range(1, model):
        pl.semaphore_signal(barrier, inc=1, device_id={"model": shifted(depth, model, step)}, device_id_type=MESH)

    outs = (og, ou)
    fetches = {}

    def fetch(key, i, *cut):
        fetches[key] = pltpu.make_async_copy(
            sources[i].at[cut] if cut else sources[i], held[i].at[cut] if cut else held[i],
            fetch_sem.at[len(fetches)],
        )

    long = wg.shape[1] // PIECES
    long_down = wd.shape[0] // PIECES
    short = wg.shape[0]
    short_down = wd.shape[1]
    units = [(a, k) for k in range(PIECES) for a in range(2)]
    count = len(units)
    work = units + [(2, k) for k in range(PIECES)]

    for u, (a, k) in enumerate(work):
        if k == 0:
            fetch(("low", a), 3 * a + 1)
            fetch(("high", a), 3 * a + 2)
        if a < 2:
            fetch(u, 3 * a, pl.ds(0, short), pl.ds(k * long, long))
        else:
            fetch(u, 3 * a, pl.ds(k * long_down, long_down), pl.ds(0, short_down))
    fetch("train", 9)
    fetch("step", 10)
    for f in fetches.values():
        f.start()

    def place(u, owner):
        a, k = units[u]
        return outs[a].at[pl.ds(k * long, long), pl.ds(pl.multiple_of(owner * short, short), short)]

    def compute(u):
        a, k = work[u]
        if k == 0:
            fetches["low", a].wait()
            fetches["high", a].wait()
        fetches[u].wait()
        if a < 2:
            w, low, high = ((wg, lg, hg), (wu, lu, hu))[a]
            cut = slice(k * long, (k + 1) * long)
            weight, low, high = w[:, cut], low[...], high[:, cut]
        else:
            cut = slice(k * long_down, (k + 1) * long_down)
            weight, low, high = wd[cut, :], ld[:, cut], hd[...]
        merged = weight.astype(jnp.float32) + mix_rate * lax.dot_general(
            low, high, (((0,), (0,)), ((), ())), preferred_element_type=jnp.float32
        )
        merged = merged.astype(jnp.bfloat16).T
        if a < 2:
            place(u, me)[...] = merged
        else:
            own[:, cut] = merged

    def copy(u, owner, send, recv, target):
        return remote(place(u, owner), place(u, owner), send, recv, target)

    def link(lane, u, owner, target):
        return copy(u, owner, link_send.at[lane, u], link_recv.at[lane, u], target)

    def across(lane, u, owner):
        return copy(u, owner, pair_send.at[lane, u], pair_recv.at[lane, u], pair)

    piece = own.shape[1] // DOWN_PIECES

    def ahead(lane, k, src, target):
        cut = (slice(None), pl.ds(k * piece, piece))
        src = own.at[cut] if src is None else early.at[(src, *cut)]
        return remote(src, early.at[(lane, *cut)], early_send.at[lane, k], early_recv.at[lane, k], target)

    def send_own(u):
        link(0, u, me, near_x).start()
        link(1, u, me, near_y).start()
        across(3, u, me).start()

    compute(0)
    fetches["train"].wait()
    fetches["step"].wait()
    norm[me, depth] = jnp.zeros(norm.shape[2:], norm.dtype)
    norm[me, depth, :, : nt.shape[1]] = nt[...] + ns[...]
    pl.semaphore_wait(barrier, rows - 1 + model - 1)
    for u in range(1, count):
        compute(u)
        send_own(u - 1)
    compute(count)
    send_own(count - 1)
    for u in range(count + 1, len(work)):
        compute(u)

    def norm_copy(step, send):
        if step < model:
            to = {"model": shifted(depth, model, step)}
            ref = norm.at[me, depth] if send else norm.at[me, shifted(depth, model, model - step)]
            slot = step - 1
        else:
            step = step - model + 1
            to = {"rows": shifted(me, rows, step)}
            ref = norm.at[me] if send else norm.at[shifted(me, rows, rows - step)]
            slot = model - 1 + step - 1
        return pltpu.make_async_remote_copy(
            src_ref=ref, dst_ref=ref, send_sem=norm_send.at[slot], recv_sem=norm_recv.at[slot],
            device_id=to, device_id_type=MESH,
        )

    for step in range(1, model):
        norm_copy(step, True).start()
    for step in range(1, model):
        norm_copy(step, False).wait_recv()
    for step in range(model, model + rows - 1):
        norm_copy(step, True).start()

    for u in range(count):
        link(0, u, near_x, near_x).wait_recv()
        if u % 2 == 0:
            link(2, u, near_x, near_y).start()
        across(0, u, near_x).start()
        link(1, u, near_y, near_y).wait_recv()
        if u % 2 == 1:
            link(2, u, near_y, near_x).start()
        across(1, u, near_y).start()

    @pl.when(at.core == 1)
    def _():
        for k in range(EARLY):
            ahead(0, k, None, near_x).start()
            ahead(1, k, None, near_y).start()

    for u in range(count):
        link(2, u, far, near_x).wait_recv()
        across(2, u, far).start()

    @pl.when(at.core == 1)
    def _():
        for k in range(EARLY):
            ahead(0, k, None, near_x).wait_recv()
            if k % 2 == 0:
                ahead(2, k, 0, near_y).start()
            ahead(1, k, None, near_y).wait_recv()
            if k % 2 == 1:
                ahead(2, k, 1, near_x).start()

    for step in range(model, model + rows - 1):
        norm_copy(step, False).wait_recv()
    for step in range(1, model + rows - 1):
        norm_copy(step, True).wait_send()
    for u in range(count):
        link(0, u, me, near_x).wait_send()
        link(1, u, me, near_y).wait_send()
        link(2, u, near_x if u % 2 == 0 else near_y, near_x).wait_send()
        for lane, mine, theirs in ((3, me, pair), (0, near_x, at.pair_x), (1, near_y, at.pair_y), (2, far, at.pair_far)):
            across(lane, u, mine).wait_send()
            across(lane, u, theirs).wait_recv()

    @pl.when(at.core == 1)
    def _():
        for k in range(EARLY):
            ahead(0, k, None, near_x).wait_send()
            ahead(1, k, None, near_y).wait_send()
            ahead(2, k, k % 2, near_x).wait_send()
            ahead(2, k, None, near_x).wait_recv()


def second_kernel(own, early, token, down, link_send, link_recv, pair_send, pair_recv, ready):
    at = Place()
    me, near_x, near_y, far, pair = at.me, at.near_x, at.near_y, at.far, at.pair
    short = own.shape[0]
    piece = own.shape[1] // DOWN_PIECES

    barrier = pltpu.get_barrier_semaphore()
    for near in (near_x, near_y):
        pl.semaphore_signal(barrier, inc=1, device_id={"rows": near}, device_id_type=MESH)
    pl.semaphore_wait(barrier, 2 + at.core)

    def cut(k):
        return slice(None), pl.ds(k * piece, piece)

    def band(owner):
        return pl.ds(pl.multiple_of(owner * short, short), short)

    def place(k, owner):
        return down.at[band(owner), pl.ds(k * piece, piece)]

    def link(lane, k, src, owner, target):
        return remote(src, place(k, owner), link_send.at[lane, k], link_recv.at[lane, k], target)

    def across(lane, k, src, owner):
        return remote(src, place(k, owner), pair_send.at[lane, k], pair_recv.at[lane, k], pair)

    def gather(first, meet):
        pieces, everything = range(first, DOWN_PIECES), range(DOWN_PIECES)
        for k in pieces:
            link(0, k, own.at[cut(k)], me, near_x).start()
            link(1, k, own.at[cut(k)], me, near_y).start()
        down[band(me), :] = own[...]

        def over():
            for k in everything:
                across(3, k, own.at[cut(k)], me).start()
            for k in range(first):
                for lane, owner in enumerate((near_x, near_y, far)):
                    across(lane, k, early.at[(lane, *cut(k))], owner).start()
            for lane, owner in enumerate((near_x, near_y, far)):
                if first:
                    down[band(owner), : first * piece] = early[lane]

        if first:
            over()
        for k in pieces:
            link(0, k, place(k, near_x), near_x, near_x).wait_recv()
            if k % 2 == 0:
                link(2, k, place(k, near_x), near_x, near_y).start()
            link(1, k, place(k, near_y), near_y, near_y).wait_recv()
            if k % 2 == 1:
                link(2, k, place(k, near_y), near_y, near_x).start()
        if not first:
            pl.semaphore_wait(ready, 1)
            over()
        for k in pieces:
            across(0, k, place(k, near_x), near_x).start()
            across(1, k, place(k, near_y), near_y).start()
        for k in pieces:
            link(2, k, place(k, far), far, near_x).wait_recv()
            across(2, k, place(k, far), far).start()

        for k in pieces:
            link(0, k, own.at[cut(k)], me, near_x).wait_send()
            link(1, k, own.at[cut(k)], me, near_y).wait_send()
            link(2, k, place(k, near_x), near_x, near_x).wait_send()
        for k in everything:
            for lane, mine, theirs in ((3, me, pair), (0, near_x, at.pair_x), (1, near_y, at.pair_y), (2, far, at.pair_far)):
                across(lane, k, place(k, mine), mine).wait_send()
                across(lane, k, place(k, theirs), theirs).wait_recv()

    @pl.when(at.core == 0)
    def _():
        pl.semaphore_signal(barrier, inc=1, device_id={"rows": pair}, device_id_type=MESH)
        gather(0, True)

    @pl.when(at.core == 1)
    def _():
        pl.semaphore_signal(ready, inc=1, device_id={"rows": pair}, device_id_type=MESH)
        gather(EARLY, False)


HBM = pl.BlockSpec(memory_space=pltpu.HBM)
VMEM = pl.BlockSpec(memory_space=pltpu.VMEM)
MIB = 2**20


def first_gather(rows, model, arrays):
    weight_gate, weight_up, weight_down, norm_train = arrays[0], arrays[3], arrays[6], arrays[9]
    own = (weight_down.shape[1], weight_down.shape[0])
    shapes = [
        (weight_gate.shape[1], weight_gate.shape[0] * rows),
        (weight_up.shape[1], weight_up.shape[0] * rows),
        own,
        (3, own[0], own[1] // DOWN_PIECES * EARLY),
    ]
    lanes = -(-norm_train.shape[1] // 128) * 128
    count = 2 * PIECES
    small = rows - 1 + model - 1
    dma = pltpu.SemaphoreType.DMA
    return pl.pallas_call(
        functools.partial(first_kernel, rows, model),
        out_shape=[pltpu.VMEM(s, jnp.bfloat16) for s in shapes] + [pltpu.VMEM((rows, model, 1, lanes), jnp.float32)],
        in_specs=[HBM] * len(arrays),
        out_specs=[VMEM] * 5,
        scratch_shapes=[pltpu.VMEM(a.shape, a.dtype) for a in arrays]
        + [
            dma((3 * PIECES + 8,)),
            dma((3, count)), dma((3, count)), dma((4, count)), dma((4, count)),
            dma((3, EARLY)), dma((3, EARLY)), dma((small,)), dma((small,)),
        ],
        compiler_params=pltpu.CompilerParams(collective_id=0, has_side_effects=True, vmem_limit_bytes=44 * MIB + MIB // 4),
    )(*arrays)


def second_gather(rows, own, early, token):
    dma = pltpu.SemaphoreType.DMA
    return pl.pallas_call(
        second_kernel,
        out_shape=pltpu.VMEM((own.shape[0] * rows, own.shape[1]), jnp.bfloat16),
        in_specs=[VMEM, VMEM, HBM],
        out_specs=VMEM,
        scratch_shapes=[
            dma((3, DOWN_PIECES)), dma((3, DOWN_PIECES)), dma((4, DOWN_PIECES)), dma((4, DOWN_PIECES)),
            pltpu.SemaphoreType.REGULAR,
        ],
        compiler_params=pltpu.CompilerParams(collective_id=1, has_side_effects=True, vmem_limit_bytes=4 * MIB),
    )(own, early, token)


def write_kernel(size, lanes, g, u, norm, og, ou, out, token, sems):
    copies = [pltpu.make_async_copy(s, t, sems.at[i]) for i, (s, t) in enumerate(((g, og), (u, ou)))]
    for c in copies:
        c.start()
    rows, model = norm.shape[:2]
    parts = [norm[r, m][:, :size] for r in range(rows) for m in range(model)]
    group = lanes // size
    packed = [jnp.concatenate(parts[i : i + group], axis=1) for i in range(0, len(parts), group)]
    out[...] = jnp.concatenate(packed, axis=0).astype(out.dtype)
    token[...] = jnp.zeros(token.shape, token.dtype)
    for c in copies:
        c.wait()


def written(size, arrays):
    lanes = arrays[2].shape[3]
    total = arrays[2].shape[0] * arrays[2].shape[1] * size
    return pl.pallas_call(
        functools.partial(write_kernel, size, lanes),
        out_shape=[jax.ShapeDtypeStruct(a.shape, a.dtype) for a in arrays[:2]]
        + [jax.ShapeDtypeStruct((total // lanes, lanes), jnp.bfloat16), jax.ShapeDtypeStruct((8, 128), jnp.float32)],
        in_specs=[VMEM] * 3,
        out_specs=[HBM] * 2 + [VMEM] * 2,
        scratch_shapes=[pltpu.SemaphoreType.DMA((2,))],
        compiler_params=pltpu.CompilerParams(vmem_limit_bytes=MIB),
    )(*arrays)


def last_kernel(d, od, sem):
    c = pltpu.make_async_copy(d, od, sem)
    c.start()
    c.wait()


def last_written(down):
    return pl.pallas_call(
        last_kernel,
        out_shape=jax.ShapeDtypeStruct(down.shape, down.dtype),
        in_specs=[VMEM],
        out_specs=HBM,
        scratch_shapes=[pltpu.SemaphoreType.DMA(())],
        compiler_params=pltpu.CompilerParams(vmem_limit_bytes=MIB),
    )(down)


def local_kernel(rows, model, *arrays):
    arrays = tuple(a.T if i in (1, 4, 7) else a for i, a in enumerate(arrays[:9])) + tuple(
        a.reshape(1, -1) for a in arrays[9:]
    )
    gate, up, own, early, norm = first_gather(rows, model, arrays)
    gate, up, serve_norm, token = written(arrays[9].shape[1], (gate, up, norm))
    down = last_written(second_gather(rows, own, early, token))
    return gate, up, down, serve_norm.reshape(-1)


def merge(weight, low, high):
    full = weight.astype(jnp.float32) + mix_rate * jnp.dot(low, high, preferred_element_type=jnp.float32)
    return full.astype(jnp.bfloat16).T


def local_plain(*arrays):
    gate, up, down = merge(*arrays[:3]), merge(*arrays[3:6]), merge(*arrays[6:9])
    return (
        lax.all_gather(gate, "rows", axis=1, tiled=True),
        lax.all_gather(up, "rows", axis=1, tiled=True),
        lax.all_gather(down, "rows", axis=0, tiled=True),
        lax.all_gather((arrays[9] + arrays[10]).astype(jnp.bfloat16), ("rows", "model"), axis=0, tiled=True),
    )


def solution(mesh):
    rows, model = mesh.shape["rows"], mesh.shape["model"]
    local = functools.partial(local_kernel, rows, model) if rows == 2 * SIDE * SIDE else local_plain
    in_specs = (
        P("rows", "model"), P("rows", None), P(None, "model"),
        P("rows", "model"), P("rows", None), P(None, "model"),
        P("model", "rows"), P("model", None), P(None, "rows"),
        P(("rows", "model")), P(("rows", "model")),
    )
    out_specs = (P("model", None), P("model", None), P(None, "model"), P())
    return jax.shard_map(local, mesh=mesh, in_specs=in_specs, out_specs=out_specs, check_vma=False)
```

time: 122 us -> 117 us (0.959)
  Pallas kernels: 121 us -> 116 us
    pallas_call x1, Pallas kernels: 9.3 us -> 6.77 us  [written(): pl.pallas_call(functools.partial(write_kernel, size, lanes), out_shape=[j...]
    pallas_call x1 -> x3, Pallas kernels: 112 us -> 110 us  [the longest x1 79.4 us: first_gather(): pl.pallas_call(functools.partial(first_kernel, rows, model), out_shape=[p...]
where the time goes in v1:
time: 117 us
  Pallas kernels  116 us (99%)
    pallas_call x1, Pallas kernels, first_gather(): pl.pallas_call(functools.partial(first_kernel, rows, model), out_shape=[p...  79.4 us
    pallas_call x1, Pallas kernels, second_gather(): pl.pallas_call(second_kernel, out_shape=pltpu.VMEM((own.shape[0] * rows,...  26.9 us
    pallas_call x1, Pallas kernels, written(): pl.pallas_call(functools.partial(write_kernel, size, lanes), out_shape=[j...  6.77 us
    pallas_call x1, Pallas kernels, last_written(): pl.pallas_call(last_kernel, out_shape=jax.ShapeDtypeStruct(down.shape, do...  3.41 us

profile of v1, /device:TPU:0, one launch (start us, length us, event | category | flops | bytes accessed | tf_op | source)
XLA Modules:
  0.0 117.1 jit_solution(4394936956619044210)
XLA Ops:
  0.6 79.4 %shard_map.138 = (bf16[2048,2048]{1,0:T(8,128)(2,1)S(1)}, bf16[2048,2048]{1,0:T(8,128)(2,1)S(1)}, bf16[256,2048]{1,0:T(8,128)(2,1)S(1)}, bf16[3,256,1536]{2,1,0:T(8,128)(2,1)S(1)}, f32[8,4,1,128]{3,2,1,0:T(1,128)S(1)}) custom-call(bf16[256,2048]{1,0:T(8,128)(2,1)} %refs_0_.1, bf16[64,256]{1,0:T(8,128)(2,1)} %bitcast.7, bf16[64,2048]{1,0:T(8,128)(2,1)} %refs_2_.1, ...), custom_call_target="tpu_custom_call" | custom-call | tf_op jit(solution)/shard_map/pallas_call | solution.py:325
  80.0 6.8 %shard_map.139 = (bf16[2048,2048]{1,0:T(8,128)(2,1)}, bf16[2048,2048]{1,0:T(8,128)(2,1)}, bf16[16,128]{1,0:T(8,128)(2,1)}, f32[8,128]{1,0:T(8,128)S(1)}) custom-call(bf16[2048,2048]{1,0:T(8,128)(2,1)S(1)} %get-tuple-element.13.g, bf16[2048,2048]{1,0:T(8,128)(2,1)S(1)} %get-tuple-element.14.u, f32[8,4,1,128]{3,2,1,0:T(1,128)S(1)} %get-tuple-element.15.norm), custom_call_target="tpu_custom_call" | custom-call | tf_op jit(solution)/shard_map/pallas_call | solution.py:372
  86.8 26.9 %shard_map.140.d = bf16[2048,2048]{1,0:T(8,128)(2,1)S(1)} custom-call(bf16[256,2048]{1,0:T(8,128)(2,1)S(1)} %get-tuple-element.18.own, bf16[3,256,1536]{2,1,0:T(8,128)(2,1)S(1)} %get-tuple-element.19.early, f32[8,128]{1,0:T(8,128)S(1)} %get-tuple-element.20.token), custom_call_target="tpu_custom_call" | custom-call | tf_op jit(solution)/shard_map/pallas_call | solution.py:342
  113.7 3.4 %shard_map.141 = bf16[2048,2048]{1,0:T(8,128)(2,1)} custom-call(bf16[2048,2048]{1,0:T(8,128)(2,1)S(1)} %shard_map.140.d), custom_call_target="tpu_custom_call" | custom-call | tf_op jit(solution)/shard_map/pallas_call | solution.py:390

commit v2 on v1

v2 whole, which is shorter than its diff:
```python
import functools

import jax
import jax.numpy as jnp
from jax import lax
from jax.experimental import pallas as pl
from jax.experimental.pallas import tpu as pltpu
from jax.sharding import PartitionSpec as P

mix_rate = 0.5
MESH = pl.DeviceIdType.MESH
UNITS = ((1, 1, 3, 3, 4, 4), (4, 4, 3, 3, 1, 1))
DOWN = (2, 2, 2, 2, 2, 2, 1, 1, 1, 1)
EARLY = 8
SIDE = 2


def cuts(parts, size):
    whole = sum(parts)
    return [(sum(parts[:i]) * size // whole, parts[i] * size // whole) for i in range(len(parts))]


class Place:
    def __init__(self):
        self.me = me = lax.axis_index("rows")
        self.core = core = lax.rem(me, 2)
        x = lax.rem(me // 2, SIDE)
        y = me // (2 * SIDE)

        def device(y, x, core):
            return (y * SIDE + x) * 2 + core

        self.near_x, self.near_y = device(y, 1 - x, core), device(1 - y, x, core)
        self.far = device(1 - y, 1 - x, core)
        self.pair = device(y, x, 1 - core)
        self.pair_x, self.pair_y = device(y, 1 - x, 1 - core), device(1 - y, x, 1 - core)
        self.pair_far = device(1 - y, 1 - x, 1 - core)


def remote(src, dst, send, recv, target):
    return pltpu.make_async_remote_copy(
        src_ref=src, dst_ref=dst, send_sem=send, recv_sem=recv,
        device_id=target if isinstance(target, dict) else {"rows": target}, device_id_type=MESH,
    )


def first_kernel(*refs):
    sources, (og, ou, own, early, norm), refs = refs[:11], refs[11:16], refs[16:]
    held, refs = refs[:11], refs[11:]
    wg, lg, hg, wu, lu, hu, wd, ld, hd, nt, ns = held
    fetch_sem, link_send, link_recv, pair_send, pair_recv, early_send, early_recv = refs
    at = Place()
    me, near_x, near_y, far, pair = at.me, at.near_x, at.near_y, at.far, at.pair

    barrier = pltpu.get_barrier_semaphore()
    for other in (near_x, near_y, pair):
        pl.semaphore_signal(barrier, inc=1, device_id={"rows": other}, device_id_type=MESH)

    outs = (og, ou)
    fetches = {}

    def fetch(key, i, *cut):
        fetches[key] = pltpu.make_async_copy(
            sources[i].at[cut] if cut else sources[i], held[i].at[cut] if cut else held[i],
            fetch_sem.at[len(fetches)],
        )

    short, short_down = wg.shape[0], wd.shape[1]
    units = [(a, *cut) for a in range(2) for cut in cuts(UNITS[a], wg.shape[1])]
    count = len(units)
    work = units + [(2, *cut) for cut in cuts((1, 1, 1, 1), wd.shape[0])]
    whole = slice(None)

    for u, (a, start, size) in enumerate(work):
        if start == 0:
            fetch(("low", a), 3 * a + 1)
            if a < 2:
                fetch(("high", a), 3 * a + 2, whole, pl.ds(0, size))
            else:
                fetch(("high", a), 3 * a + 2)
        if a < 2:
            fetch(u, 3 * a, whole, pl.ds(start, size))
        else:
            fetch(u, 3 * a, pl.ds(start, size), whole)
        if start == 0 and a < 2:
            fetch(("rest", a), 3 * a + 2, whole, pl.ds(size, wg.shape[1] - size))
    fetch("train", 9)
    fetch("step", 10)
    for f in fetches.values():
        f.start()

    def place(u, owner):
        a, start, size = units[u]
        return outs[a].at[pl.ds(start, size), pl.ds(pl.multiple_of(owner * short, short), short)]

    def compute(u):
        a, start, size = work[u]
        if start == 0:
            fetches["low", a].wait()
            fetches["high", a].wait()
        elif a < 2 and work[u - 1][1] == 0:
            fetches["rest", a].wait()
        fetches[u].wait()
        cut = slice(start, start + size)
        if a < 2:
            w, low, high = ((wg, lg, hg), (wu, lu, hu))[a]
            weight, low, high = w[:, cut], low[...], high[:, cut]
        else:
            weight, low, high = wd[cut, :], ld[:, cut], hd[...]
        merged = weight.astype(jnp.float32) + mix_rate * lax.dot_general(
            low, high, (((0,), (0,)), ((), ())), preferred_element_type=jnp.float32
        )
        merged = merged.astype(jnp.bfloat16).T
        if a < 2:
            place(u, me)[...] = merged
        else:
            own[:, cut] = merged

    def copy(u, owner, send, recv, target):
        return remote(place(u, owner), place(u, owner), send, recv, target)

    def link(lane, u, owner, target):
        return copy(u, owner, link_send.at[lane, u], link_recv.at[lane, u], target)

    def across(lane, u, owner):
        return copy(u, owner, pair_send.at[lane, u], pair_recv.at[lane, u], pair)

    pieces = cuts(DOWN, own.shape[1])[:EARLY]

    def ahead(lane, k, src, target):
        cut = (whole, pl.ds(*pieces[k]))
        src = own.at[cut] if src is None else early.at[(src, *cut)]
        return remote(src, early.at[(lane, *cut)], early_send.at[lane, k], early_recv.at[lane, k], target)

    def send_own(u):
        link(0, u, me, near_x).start()
        link(1, u, me, near_y).start()
        across(3, u, me).start()

    compute(0)
    pl.semaphore_wait(barrier, 3)
    for u in range(1, count + 1):
        compute(u)
        send_own(u - 1)
    for u in range(count + 1, len(work)):
        compute(u)
    fetches["train"].wait()
    fetches["step"].wait()
    norm[...] = jnp.zeros(norm.shape, norm.dtype)
    norm[:, : nt.shape[1]] = nt[...] + ns[...]

    for u in range(count):
        link(0, u, near_x, near_x).wait_recv()
        if u % 2 == 0:
            link(2, u, near_x, near_y).start()
        across(0, u, near_x).start()
        link(1, u, near_y, near_y).wait_recv()
        if u % 2 == 1:
            link(2, u, near_y, near_x).start()
        across(1, u, near_y).start()

    @pl.when(at.core == 1)
    def _():
        for k in range(EARLY):
            ahead(0, k, None, near_x).start()
            ahead(1, k, None, near_y).start()

    for u in range(count):
        link(2, u, far, near_x).wait_recv()
        across(2, u, far).start()

    @pl.when(at.core == 1)
    def _():
        for k in range(EARLY):
            ahead(0, k, None, near_x).wait_recv()
            if k % 2 == 0:
                ahead(2, k, 0, near_y).start()
            ahead(1, k, None, near_y).wait_recv()
            if k % 2 == 1:
                ahead(2, k, 1, near_x).start()

    for u in range(count):
        link(0, u, me, near_x).wait_send()
        link(1, u, me, near_y).wait_send()
        link(2, u, near_x, near_x).wait_send()
        for lane, mine, theirs in ((3, me, pair), (0, near_x, at.pair_x), (1, near_y, at.pair_y), (2, far, at.pair_far)):
            across(lane, u, mine).wait_send()
            across(lane, u, theirs).wait_recv()

    @pl.when(at.core == 1)
    def _():
        for k in range(EARLY):
            ahead(0, k, None, near_x).wait_send()
            ahead(1, k, None, near_y).wait_send()
            ahead(2, k, k % 2, near_x).wait_send()
            ahead(2, k, None, near_x).wait_recv()


def second_kernel(model, own, early, part, token, down, norm, *sems):
    link_send, link_recv, pair_send, pair_recv, norm_send, norm_recv, ready = sems
    at = Place()
    me, near_x, near_y, far, pair = at.me, at.near_x, at.near_y, at.far, at.pair
    depth = lax.axis_index("model")
    short = own.shape[0]
    pieces = cuts(DOWN, own.shape[1])

    barrier = pltpu.get_barrier_semaphore()
    for other in (near_x, near_y, far):
        pl.semaphore_signal(barrier, inc=1, device_id={"rows": other}, device_id_type=MESH)
    for step in range(1, model):
        pl.semaphore_signal(barrier, inc=1, device_id={"model": lax.rem(depth + step, model)}, device_id_type=MESH)
    norm[me, depth] = part[...]
    pl.semaphore_wait(barrier, 2 + model + at.core)

    def cut(k):
        return slice(None), pl.ds(*pieces[k])

    def band(owner):
        return pl.ds(pl.multiple_of(owner * short, short), short)

    def place(k, owner):
        return down.at[band(owner), pl.ds(*pieces[k])]

    def link(lane, k, src, owner, target):
        return remote(src, place(k, owner), link_send.at[lane, k], link_recv.at[lane, k], target)

    def across(lane, k, src, owner):
        return remote(src, place(k, owner), pair_send.at[lane, k], pair_recv.at[lane, k], pair)

    def norm_copy(slot, ref, target):
        return remote(ref, ref, norm_send.at[slot], norm_recv.at[slot], target)

    rings = range(1, model)
    rows_mine = ((me, pair), (near_x, at.pair_x), (near_y, at.pair_y), (far, at.pair_far))

    def norm_deep(step):
        return norm_copy(step - 1, norm.at[me, depth], {"model": lax.rem(depth + step, model)})

    def norm_deep_back(step):
        return norm_copy(step - 1, norm.at[me, lax.rem(depth + model - step, model)], {"model": lax.rem(depth + step, model)})

    def norm_wide(lane, owner, target):
        return norm_copy(model - 1 + lane, norm.at[owner], target)

    def norm_across(lane, owner):
        return norm_copy(model + 2 + lane, norm.at[owner], pair)

    def gather(first):
        late, everything = range(first, len(pieces)), range(len(pieces))
        for k in late:
            link(0, k, own.at[cut(k)], me, near_x).start()
            link(1, k, own.at[cut(k)], me, near_y).start()
        for step in rings:
            norm_deep(step).start()

        def over():
            for k in everything:
                across(3, k, own.at[cut(k)], me).start()
            for k in range(first):
                for lane, owner in enumerate((near_x, near_y, far)):
                    across(lane, k, early.at[(lane, *cut(k))], owner).start()

        def spread():
            for step in rings:
                norm_deep_back(step).wait_recv()
            for lane, owner in enumerate((near_x, near_y, far)):
                norm_wide(lane, me, owner).start()

        if first:
            over()
        down[band(me), :] = own[...]
        if first:
            end = sum(pieces[first - 1])
            for lane, owner in enumerate((near_x, near_y, far)):
                down[band(owner), :end] = early[lane]
        for k in late:
            link(0, k, place(k, near_x), near_x, near_x).wait_recv()
            if k % 2 == 0:
                link(2, k, place(k, near_x), near_x, near_y).start()
            link(1, k, place(k, near_y), near_y, near_y).wait_recv()
            if k % 2 == 1:
                link(2, k, place(k, near_y), near_y, near_x).start()
            if k == first + 1:
                spread()
        if not first:
            pl.semaphore_wait(ready, 1)
            over()
        for k in late:
            across(0, k, place(k, near_x), near_x).start()
            across(1, k, place(k, near_y), near_y).start()
        for lane, owner in enumerate((near_x, near_y, far)):
            norm_wide(lane, owner, owner).wait_recv()
        for lane, (mine, _) in enumerate(rows_mine):
            norm_across(lane, mine).start()
        for k in late:
            link(2, k, place(k, far), far, near_x).wait_recv()
            across(2, k, place(k, far), far).start()

        for step in rings:
            norm_deep(step).wait_send()
        for lane, owner in enumerate((near_x, near_y, far)):
            norm_wide(lane, me, owner).wait_send()
        for lane, (mine, theirs) in enumerate(rows_mine):
            norm_across(lane, mine).wait_send()
            norm_across(lane, theirs).wait_recv()
        for k in late:
            link(0, k, own.at[cut(k)], me, near_x).wait_send()
            link(1, k, own.at[cut(k)], me, near_y).wait_send()
            link(2, k, place(k, near_x), near_x, near_x).wait_send()
        for k in everything:
            for lane, mine, theirs in ((3, me, pair), (0, near_x, at.pair_x), (1, near_y, at.pair_y), (2, far, at.pair_far)):
                across(lane, k, place(k, mine), mine).wait_send()
                across(lane, k, place(k, theirs), theirs).wait_recv()

    @pl.when(at.core == 0)
    def _():
        pl.semaphore_signal(barrier, inc=1, device_id={"rows": pair}, device_id_type=MESH)
        gather(0)

    @pl.when(at.core == 1)
    def _():
        pl.semaphore_signal(ready, inc=1, device_id={"rows": pair}, device_id_type=MESH)
        gather(EARLY)


HBM = pl.BlockSpec(memory_space=pltpu.HBM)
VMEM = pl.BlockSpec(memory_space=pltpu.VMEM)
MIB = 2**20


def first_gather(rows, arrays):
    weight_gate, weight_up, weight_down, norm_train = arrays[0], arrays[3], arrays[6], arrays[9]
    own = (weight_down.shape[1], weight_down.shape[0])
    shapes = [
        (weight_gate.shape[1], weight_gate.shape[0] * rows),
        (weight_up.shape[1], weight_up.shape[0] * rows),
        own,
        (3, own[0], sum(cuts(DOWN, own[1])[EARLY - 1])),
    ]
    lanes = -(-norm_train.shape[1] // 128) * 128
    count = len(UNITS[0]) + len(UNITS[1])
    dma = pltpu.SemaphoreType.DMA
    return pl.pallas_call(
        first_kernel,
        out_shape=[pltpu.VMEM(s, jnp.bfloat16) for s in shapes] + [pltpu.VMEM((1, lanes), jnp.float32)],
        in_specs=[HBM] * len(arrays),
        out_specs=[VMEM] * 5,
        scratch_shapes=[pltpu.VMEM(a.shape, a.dtype) for a in arrays]
        + [
            dma((count + 14,)),
            dma((3, count)), dma((3, count)), dma((4, count)), dma((4, count)),
            dma((3, EARLY)), dma((3, EARLY)),
        ],
        compiler_params=pltpu.CompilerParams(collective_id=0, has_side_effects=True, vmem_limit_bytes=44 * MIB),
    )(*arrays)


def second_gather(rows, model, own, early, part, token):
    dma = pltpu.SemaphoreType.DMA
    count = len(DOWN)
    small = model - 1 + 3 + 4
    return pl.pallas_call(
        functools.partial(second_kernel, model),
        out_shape=[
            pltpu.VMEM((own.shape[0] * rows, own.shape[1]), jnp.bfloat16),
            pltpu.VMEM((rows, model, *part.shape), jnp.float32),
        ],
        in_specs=[VMEM, VMEM, VMEM, HBM],
        out_specs=[VMEM, VMEM],
        scratch_shapes=[
            dma((3, count)), dma((3, count)), dma((4, count)), dma((4, count)), dma((small,)), dma((small,)),
            pltpu.SemaphoreType.REGULAR,
        ],
        compiler_params=pltpu.CompilerParams(collective_id=1, has_side_effects=True, vmem_limit_bytes=4 * MIB),
    )(own, early, part, token)


def write_kernel(g, u, og, ou, token, sems):
    copies = [pltpu.make_async_copy(s, t, sems.at[i]) for i, (s, t) in enumerate(((g, og), (u, ou)))]
    for c in copies:
        c.start()
    token[...] = jnp.zeros(token.shape, token.dtype)
    for c in copies:
        c.wait()


def written(gate, up):
    return pl.pallas_call(
        write_kernel,
        out_shape=[jax.ShapeDtypeStruct(a.shape, a.dtype) for a in (gate, up)]
        + [jax.ShapeDtypeStruct((8, 128), jnp.float32)],
        in_specs=[VMEM] * 2,
        out_specs=[HBM] * 2 + [VMEM],
        scratch_shapes=[pltpu.SemaphoreType.DMA((2,))],
        compiler_params=pltpu.CompilerParams(vmem_limit_bytes=MIB),
    )(gate, up)


def last_kernel(size, d, norm, od, out, packed_norm, sems):
    c = pltpu.make_async_copy(d, od, sems.at[0])
    c.start()
    rows, model, _, lanes = norm.shape
    parts = [norm[r, m][:, :size] for r in range(rows) for m in range(model)]
    group = lanes // size
    packed = [jnp.concatenate(parts[i : i + group], axis=1) for i in range(0, len(parts), group)]
    packed_norm[...] = jnp.concatenate(packed, axis=0).astype(out.dtype)
    small = pltpu.make_async_copy(packed_norm, out, sems.at[1])
    small.start()
    small.wait()
    c.wait()


def last_written(size, down, norm):
    rows, model, _, lanes = norm.shape
    packed = (rows * model * size // lanes, lanes)
    return pl.pallas_call(
        functools.partial(last_kernel, size),
        out_shape=[jax.ShapeDtypeStruct(down.shape, down.dtype), jax.ShapeDtypeStruct(packed, jnp.bfloat16)],
        in_specs=[VMEM] * 2,
        out_specs=[HBM] * 2,
        scratch_shapes=[pltpu.VMEM(packed, jnp.bfloat16), pltpu.SemaphoreType.DMA((2,))],
        compiler_params=pltpu.CompilerParams(vmem_limit_bytes=MIB),
    )(down, norm)


def local_kernel(rows, model, *arrays):
    arrays = tuple(a.T if i in (1, 4, 7) else a for i, a in enumerate(arrays[:9])) + tuple(
        a.reshape(1, -1) for a in arrays[9:]
    )
    gate, up, own, early, part = first_gather(rows, arrays)
    gate, up, token = written(gate, up)
    down, norm = second_gather(rows, model, own, early, part, token)
    down, serve_norm = last_written(arrays[9].shape[1], down, norm)
    return gate, up, down, serve_norm.reshape(-1)


def merge(weight, low, high):
    full = weight.astype(jnp.float32) + mix_rate * jnp.dot(low, high, preferred_element_type=jnp.float32)
    return full.astype(jnp.bfloat16).T


def local_plain(*arrays):
    gate, up, down = merge(*arrays[:3]), merge(*arrays[3:6]), merge(*arrays[6:9])
    return (
        lax.all_gather(gate, "rows", axis=1, tiled=True),
        lax.all_gather(up, "rows", axis=1, tiled=True),
        lax.all_gather(down, "rows", axis=0, tiled=True),
        lax.all_gather((arrays[9] + arrays[10]).astype(jnp.bfloat16), ("rows", "model"), axis=0, tiled=True),
    )


def solution(mesh):
    rows, model = mesh.shape["rows"], mesh.shape["model"]
    local = functools.partial(local_kernel, rows, model) if rows == 2 * SIDE * SIDE else local_plain
    in_specs = (
        P("rows", "model"), P("rows", None), P(None, "model"),
        P("rows", "model"), P("rows", None), P(None, "model"),
        P("model", "rows"), P("model", None), P(None, "rows"),
        P(("rows", "model")), P(("rows", "model")),
    )
    out_specs = (P("model", None), P("model", None), P(None, "model"), P())
    return jax.shard_map(local, mesh=mesh, in_specs=in_specs, out_specs=out_specs, check_vma=False)
```

time: 117 us -> 115 us (0.983)
  Pallas kernels: 116 us -> 114 us
    pallas_call x4, Pallas kernels: 116 us -> 114 us  [the longest x1 76.9 us: first_gather(): pl.pallas_call(first_kernel, out_shape=[pltpu.VMEM(s, jnp.bfloat16) for s...]
where the time goes in v2:
time: 115 us
  Pallas kernels  114 us (99%)
    pallas_call x1, Pallas kernels, first_gather(): pl.pallas_call(first_kernel, out_shape=[pltpu.VMEM(s, jnp.bfloat16) for s...  76.9 us
    pallas_call x1, Pallas kernels, second_gather(): pl.pallas_call(functools.partial(second_kernel, model), out_shape=[pltpu....  27.8 us
    pallas_call x1, Pallas kernels, written(): pl.pallas_call(write_kernel, out_shape=[jax.ShapeDtypeStruct(a.shape, a.d...  6.18 us
    pallas_call x1, Pallas kernels, last_written(): pl.pallas_call(functools.partial(last_kernel, size), out_shape=[jax.Shape...  3.42 us

profile of v2, /device:TPU:0, one launch (start us, length us, event | category | flops | bytes accessed | tf_op | source)
XLA Modules:
  0.0 115.0 jit_solution(10399368639144266681)
XLA Ops:
  0.6 76.9 %shard_map.138 = (bf16[2048,2048]{1,0:T(8,128)(2,1)S(1)}, bf16[2048,2048]{1,0:T(8,128)(2,1)S(1)}, bf16[256,2048]{1,0:T(8,128)(2,1)S(1)}, bf16[3,256,1792]{2,1,0:T(8,128)(2,1)S(1)}, f32[1,128]{1,0:T(1,128)S(1)}) custom-call(bf16[256,2048]{1,0:T(8,128)(2,1)} %refs_0_.1, bf16[64,256]{1,0:T(8,128)(2,1)} %bitcast.7, bf16[64,2048]{1,0:T(8,128)(2,1)} %refs_2_.1, ...), custom_call_target="tpu_custom_call" | custom-call | tf_op jit(solution)/shard_map/pallas_call | solution.py:343
  77.5 6.2 %shard_map.139 = (bf16[2048,2048]{1,0:T(8,128)(2,1)}, bf16[2048,2048]{1,0:T(8,128)(2,1)}, f32[8,128]{1,0:T(8,128)S(1)}) custom-call(bf16[2048,2048]{1,0:T(8,128)(2,1)S(1)} %get-tuple-element.16.g, bf16[2048,2048]{1,0:T(8,128)(2,1)S(1)} %get-tuple-element.17.u), custom_call_target="tpu_custom_call" | custom-call | tf_op jit(solution)/shard_map/pallas_call | solution.py:388
  83.7 27.8 %shard_map.140 = (bf16[2048,2048]{1,0:T(8,128)(2,1)S(1)}, f32[8,4,1,128]{3,2,1,0:T(1,128)S(1)}) custom-call(bf16[256,2048]{1,0:T(8,128)(2,1)S(1)} %get-tuple-element.20.own, bf16[3,256,1792]{2,1,0:T(8,128)(2,1)S(1)} %get-tuple-element.21.early, f32[1,128]{1,0:T(1,128)S(1)} %get-tuple-element.22.part, f32[8,128]{1,0:T(8,128)S(1)} %get-tuple-element.23.token), custom_call_target="tpu_custom_call" | custom-call | tf_op jit(solution)/shard_map/pallas_call | solution.py:362
  111.6 3.4 %shard_map.141 = (bf16[2048,2048]{1,0:T(8,128)(2,1)}, bf16[16,128]{1,0:T(8,128)(2,1)}) custom-call(bf16[2048,2048]{1,0:T(8,128)(2,1)S(1)} %get-tuple-element.24.d, f32[8,4,1,128]{3,2,1,0:T(1,128)S(1)} %get-tuple-element.25.norm), custom_call_target="tpu_custom_call" | custom-call | tf_op jit(solution)/shard_map/pallas_call | solution.py:416

commit v3 on v2

--- a/solution.py
+++ b/solution.py
@@ -10,8 +10,8 @@
 mix_rate = 0.5
 MESH = pl.DeviceIdType.MESH
 UNITS = ((1, 1, 3, 3, 4, 4), (4, 4, 3, 3, 1, 1))
-DOWN = (2, 2, 2, 2, 2, 2, 1, 1, 1, 1)
-EARLY = 8
+DOWN = (4, 4, 3, 3, 1, 1)
+EARLY = 4
 SIDE = 2
 
 
@@ -44,17 +44,24 @@
     )
 
 
-def first_kernel(*refs):
+def first_kernel(model, *refs):
     sources, (og, ou, own, early, norm), refs = refs[:11], refs[11:16], refs[16:]
     held, refs = refs[:11], refs[11:]
     wg, lg, hg, wu, lu, hu, wd, ld, hd, nt, ns = held
-    fetch_sem, link_send, link_recv, pair_send, pair_recv, early_send, early_recv = refs
+    fetch_sem, link_send, link_recv, pair_send, pair_recv, early_send, early_recv, norm_send, norm_recv, part = refs
     at = Place()
     me, near_x, near_y, far, pair = at.me, at.near_x, at.near_y, at.far, at.pair
+    depth = lax.axis_index("model")
+    chip = me // 2
 
     barrier = pltpu.get_barrier_semaphore()
     for other in (near_x, near_y, pair):
         pl.semaphore_signal(barrier, inc=1, device_id={"rows": other}, device_id_type=MESH)
+
+    @pl.when(at.core == 1)
+    def _():
+        for step in range(1, model):
+            pl.semaphore_signal(barrier, inc=1, device_id={"model": lax.rem(depth + step, model)}, device_id_type=MESH)
 
     outs = (og, ou)
     fetches = {}
@@ -138,7 +145,7 @@
         across(3, u, me).start()
 
     compute(0)
-    pl.semaphore_wait(barrier, 3)
+    pl.semaphore_wait(barrier, 3 + at.core * (model - 1))
     for u in range(1, count + 1):
         compute(u)
         send_own(u - 1)
@@ -146,8 +153,48 @@
         compute(u)
     fetches["train"].wait()
     fetches["step"].wait()
-    norm[...] = jnp.zeros(norm.shape, norm.dtype)
-    norm[:, : nt.shape[1]] = nt[...] + ns[...]
+    part[...] = jnp.zeros(part.shape, part.dtype)
+    part[:, : nt.shape[1]] = nt[...] + ns[...]
+
+    @pl.when(at.core == 1)
+    def _():
+        norm[chip, depth, 1] = part[...]
+
+    def norm_copy(slot, ref, target):
+        return remote(ref, ref, norm_send.at[slot], norm_recv.at[slot], target)
+
+    def norm_part():
+        return remote(part, norm.at[chip, depth, 0], norm_send.at[0], norm_recv.at[0], pair)
+
+    def norm_deep(step, send):
+        return norm_copy(
+            step, norm.at[chip, depth if send else lax.rem(depth + model - step, model)],
+            {"model": lax.rem(depth + step, model)},
+        )
+
+    def norm_wide(lane, owner, target):
+        return norm_copy(model + lane, norm.at[owner // 2], target)
+
+    def norm_whole():
+        return norm_copy(model + 3, norm, pair)
+
+    def norm_step(u):
+        if u == 1:
+            norm_part().wait_recv()
+            for step in range(1, model):
+                norm_deep(step, True).start()
+        if u == 2:
+            for step in range(1, model):
+                norm_deep(step, False).wait_recv()
+            norm_wide(0, me, near_x).start()
+            norm_wide(1, me, near_y).start()
+        if u == 3:
+            norm_wide(0, near_x, near_x).wait_recv()
+            norm_wide(1, near_y, near_y).wait_recv()
+            norm_wide(2, near_x, near_y).start()
+        if u == 4:
+            norm_wide(2, far, near_y).wait_recv()
+            norm_whole().start()
 
     for u in range(count):
         link(0, u, near_x, near_x).wait_recv()
@@ -158,6 +205,10 @@
         if u % 2 == 1:
             link(2, u, near_y, near_x).start()
         across(1, u, near_y).start()
+        if u == 0:
+            pl.when(at.core == 0)(lambda: norm_part().start())
+        if 1 <= u <= 4:
+            pl.when(at.core == 1)(functools.partial(norm_step, u))
 
     @pl.when(at.core == 1)
     def _():
@@ -179,6 +230,11 @@
             if k % 2 == 1:
                 ahead(2, k, 1, near_x).start()
 
+    @pl.when(at.core == 0)
+    def _():
+        norm_part().wait_send()
+        norm_whole().wait_recv()
+
     for u in range(count):
         link(0, u, me, near_x).wait_send()
         link(1, u, me, near_y).wait_send()
@@ -194,23 +250,24 @@
             ahead(1, k, None, near_y).wait_send()
             ahead(2, k, k % 2, near_x).wait_send()
             ahead(2, k, None, near_x).wait_recv()
-
-
-def second_kernel(model, own, early, part, token, down, norm, *sems):
-    link_send, link_recv, pair_send, pair_recv, norm_send, norm_recv, ready = sems
+        for step in range(1, model):
+            norm_deep(step, True).wait_send()
+        norm_wide(0, me, near_x).wait_send()
+        norm_wide(1, me, near_y).wait_send()
+        norm_wide(2, near_x, near_y).wait_send()
+        norm_whole().wait_send()
+
+
+def second_kernel(own, early, token, down, link_send, link_recv, pair_send, pair_recv, ready):
     at = Place()
     me, near_x, near_y, far, pair = at.me, at.near_x, at.near_y, at.far, at.pair
-    depth = lax.axis_index("model")
     short = own.shape[0]
     pieces = cuts(DOWN, own.shape[1])
 
     barrier = pltpu.get_barrier_semaphore()
-    for other in (near_x, near_y, far):
+    for other in (near_x, near_y):
         pl.semaphore_signal(barrier, inc=1, device_id={"rows": other}, device_id_type=MESH)
-    for step in range(1, model):
-        pl.semaphore_signal(barrier, inc=1, device_id={"model": lax.rem(depth + step, model)}, device_id_type=MESH)
-    norm[me, depth] = part[...]
-    pl.semaphore_wait(barrier, 2 + model + at.core)
+    pl.semaphore_wait(barrier, 2 + at.core)
 
     def cut(k):
         return slice(None), pl.ds(*pieces[k])
@@ -226,32 +283,12 @@
 
     def across(lane, k, src, owner):
         return remote(src, place(k, owner), pair_send.at[lane, k], pair_recv.at[lane, k], pair)
-
-    def norm_copy(slot, ref, target):
-        return remote(ref, ref, norm_send.at[slot], norm_recv.at[slot], target)
-
-    rings = range(1, model)
-    rows_mine = ((me, pair), (near_x, at.pair_x), (near_y, at.pair_y), (far, at.pair_far))
-
-    def norm_deep(step):
-        return norm_copy(step - 1, norm.at[me, depth], {"model": lax.rem(depth + step, model)})
-
-    def norm_deep_back(step):
-        return norm_copy(step - 1, norm.at[me, lax.rem(depth + model - step, model)], {"model": lax.rem(depth + step, model)})
-
-    def norm_wide(lane, owner, target):
-        return norm_copy(model - 1 + lane, norm.at[owner], target)
-
-    def norm_across(lane, owner):
-        return norm_copy(model + 2 + lane, norm.at[owner], pair)
 
     def gather(first):
         late, everything = range(first, len(pieces)), range(len(pieces))
         for k in late:
             link(0, k, own.at[cut(k)], me, near_x).start()
             link(1, k, own.at[cut(k)], me, near_y).start()
-        for step in rings:
-            norm_deep(step).start()
 
         def over():
             for k in everything:
@@ -259,12 +296,6 @@
             for k in range(first):
                 for lane, owner in enumerate((near_x, near_y, far)):
                     across(lane, k, early.at[(lane, *cut(k))], owner).start()
-
-        def spread():
-            for step in rings:
-                norm_deep_back(step).wait_recv()
-            for lane, owner in enumerate((near_x, near_y, far)):
-                norm_wide(lane, me, owner).start()
 
         if first:
             over()
@@ -280,29 +311,16 @@
             link(1, k, place(k, near_y), near_y, near_y).wait_recv()
             if k % 2 == 1:
                 link(2, k, place(k, near_y), near_y, near_x).start()
-            if k == first + 1:
-                spread()
         if not first:
             pl.semaphore_wait(ready, 1)
             over()
         for k in late:
             across(0, k, place(k, near_x), near_x).start()
             across(1, k, place(k, near_y), near_y).start()
-        for lane, owner in enumerate((near_x, near_y, far)):
-            norm_wide(lane, owner, owner).wait_recv()
-        for lane, (mine, _) in enumerate(rows_mine):
-            norm_across(lane, mine).start()
         for k in late:
             link(2, k, place(k, far), far, near_x).wait_recv()
             across(2, k, place(k, far), far).start()
 
-        for step in rings:
-            norm_deep(step).wait_send()
-        for lane, owner in enumerate((near_x, near_y, far)):
-            norm_wide(lane, me, owner).wait_send()
-        for lane, (mine, theirs) in enumerate(rows_mine):
-            norm_across(lane, mine).wait_send()
-            norm_across(lane, theirs).wait_recv()
         for k in late:
             link(0, k, own.at[cut(k)], me, near_x).wait_send()
             link(1, k, own.at[cut(k)], me, near_y).wait_send()
@@ -328,7 +346,7 @@
 MIB = 2**20
 
 
-def first_gather(rows, arrays):
+def first_gather(rows, model, arrays):
     weight_gate, weight_up, weight_down, norm_train = arrays[0], arrays[3], arrays[6], arrays[9]
     own = (weight_down.shape[1], weight_down.shape[0])
     shapes = [
@@ -341,96 +359,89 @@
     count = len(UNITS[0]) + len(UNITS[1])
     dma = pltpu.SemaphoreType.DMA
     return pl.pallas_call(
-        first_kernel,
-        out_shape=[pltpu.VMEM(s, jnp.bfloat16) for s in shapes] + [pltpu.VMEM((1, lanes), jnp.float32)],
+        functools.partial(first_kernel, model),
+        out_shape=[pltpu.VMEM(s, jnp.bfloat16) for s in shapes] + [pltpu.VMEM((rows // 2, model, 2, 1, lanes), jnp.float32)],
         in_specs=[HBM] * len(arrays),
         out_specs=[VMEM] * 5,
         scratch_shapes=[pltpu.VMEM(a.shape, a.dtype) for a in arrays]
         + [
             dma((count + 14,)),
             dma((3, count)), dma((3, count)), dma((4, count)), dma((4, count)),
-            dma((3, EARLY)), dma((3, EARLY)),
+            dma((3, EARLY)), dma((3, EARLY)), dma((model + 4,)), dma((model + 4,)),
+            pltpu.VMEM((1, lanes), jnp.float32),
         ],
         compiler_params=pltpu.CompilerParams(collective_id=0, has_side_effects=True, vmem_limit_bytes=44 * MIB),
     )(*arrays)
 
 
-def second_gather(rows, model, own, early, part, token):
+def second_gather(rows, own, early, token):
     dma = pltpu.SemaphoreType.DMA
     count = len(DOWN)
-    small = model - 1 + 3 + 4
     return pl.pallas_call(
-        functools.partial(second_kernel, model),
-        out_shape=[
-            pltpu.VMEM((own.shape[0] * rows, own.shape[1]), jnp.bfloat16),
-            pltpu.VMEM((rows, model, *part.shape), jnp.float32),
-        ],
-        in_specs=[VMEM, VMEM, VMEM, HBM],
-        out_specs=[VMEM, VMEM],
+        second_kernel,
+        out_shape=pltpu.VMEM((own.shape[0] * rows, own.shape[1]), jnp.bfloat16),
+        in_specs=[VMEM, VMEM, HBM],
+        out_specs=VMEM,
         scratch_shapes=[
-            dma((3, count)), dma((3, count)), dma((4, count)), dma((4, count)), dma((small,)), dma((small,)),
-            pltpu.SemaphoreType.REGULAR,
+            dma((3, count)), dma((3, count)), dma((4, count)), dma((4, count)), pltpu.SemaphoreType.REGULAR,
         ],
         compiler_params=pltpu.CompilerParams(collective_id=1, has_side_effects=True, vmem_limit_bytes=4 * MIB),
-    )(own, early, part, token)
-
-
-def write_kernel(g, u, og, ou, token, sems):
-    copies = [pltpu.make_async_copy(s, t, sems.at[i]) for i, (s, t) in enumerate(((g, og), (u, ou)))]
-    for c in copies:
-        c.start()
+    )(own, early, token)
+
+
+def write_kernel(size, g, u, norm, og, ou, out, token, packed_norm, sems):
+    copies = [pltpu.make_async_copy(s, t, sems.at[i]) for i, (s, t) in enumerate(((g, og), (u, ou), (packed_norm, out)))]
+    copies[0].start()
+    copies[1].start()
     token[...] = jnp.zeros(token.shape, token.dtype)
-    for c in copies:
-        c.wait()
-
-
-def written(gate, up):
-    return pl.pallas_call(
-        write_kernel,
-        out_shape=[jax.ShapeDtypeStruct(a.shape, a.dtype) for a in (gate, up)]
-        + [jax.ShapeDtypeStruct((8, 128), jnp.float32)],
-        in_specs=[VMEM] * 2,
-        out_specs=[HBM] * 2 + [VMEM],
-        scratch_shapes=[pltpu.SemaphoreType.DMA((2,))],
-        compiler_params=pltpu.CompilerParams(vmem_limit_bytes=MIB),
-    )(gate, up)
-
-
-def last_kernel(size, d, norm, od, out, packed_norm, sems):
-    c = pltpu.make_async_copy(d, od, sems.at[0])
-    c.start()
-    rows, model, _, lanes = norm.shape
-    parts = [norm[r, m][:, :size] for r in range(rows) for m in range(model)]
+    chips, model, cores, _, lanes = norm.shape
+    parts = [norm[r, m, c][:, :size] for r in range(chips) for c in range(cores) for m in range(model)]
     group = lanes // size
     packed = [jnp.concatenate(parts[i : i + group], axis=1) for i in range(0, len(parts), group)]
     packed_norm[...] = jnp.concatenate(packed, axis=0).astype(out.dtype)
-    small = pltpu.make_async_copy(packed_norm, out, sems.at[1])
-    small.start()
-    small.wait()
+    copies[2].start()
+    for c in copies:
+        c.wait()
+
+
+def written(size, gate, up, norm):
+    chips, model, cores, _, lanes = norm.shape
+    packed = (chips * model * cores * size // lanes, lanes)
+    return pl.pallas_call(
+        functools.partial(write_kernel, size),
+        out_shape=[jax.ShapeDtypeStruct(s, jnp.bfloat16) for s in (gate.shape, up.shape, packed)]
+        + [jax.ShapeDtypeStruct((8, 128), jnp.float32)],
+        in_specs=[VMEM] * 3,
+        out_specs=[HBM] * 3 + [VMEM],
+        scratch_shapes=[pltpu.VMEM(packed, jnp.bfloat16), pltpu.SemaphoreType.DMA((3,))],
+        compiler_params=pltpu.CompilerParams(vmem_limit_bytes=MIB),
+    )(gate, up, norm)
+
+
+def last_kernel(d, od, sem):
+    c = pltpu.make_async_copy(d, od, sem)
+    c.start()
     c.wait()
 
 
-def last_written(size, down, norm):
-    rows, model, _, lanes = norm.shape
-    packed = (rows * model * size // lanes, lanes)
+def last_written(down):
     return pl.pallas_call(
-        functools.partial(last_kernel, size),
-        out_shape=[jax.ShapeDtypeStruct(down.shape, down.dtype), jax.ShapeDtypeStruct(packed, jnp.bfloat16)],
-        in_specs=[VMEM] * 2,
-        out_specs=[HBM] * 2,
-        scratch_shapes=[pltpu.VMEM(packed, jnp.bfloat16), pltpu.SemaphoreType.DMA((2,))],
+        last_kernel,
+        out_shape=jax.ShapeDtypeStruct(down.shape, down.dtype),
+        in_specs=[VMEM],
+        out_specs=HBM,
+        scratch_shapes=[pltpu.SemaphoreType.DMA(())],
         compiler_params=pltpu.CompilerParams(vmem_limit_bytes=MIB),
-    )(down, norm)
+    )(down)
 
 
 def local_kernel(rows, model, *arrays):
     arrays = tuple(a.T if i in (1, 4, 7) else a for i, a in enumerate(arrays[:9])) + tuple(
         a.reshape(1, -1) for a in arrays[9:]
     )
-    gate, up, own, early, part = first_gather(rows, arrays)
-    gate, up, token = written(gate, up)
-    down, norm = second_gather(rows, model, own, early, part, token)
-    down, serve_norm = last_written(arrays[9].shape[1], down, norm)
+    gate, up, own, early, norm = first_gather(rows, model, arrays)
+    gate, up, serve_norm, token = written(arrays[9].shape[1], gate, up, norm)
+    down = last_written(second_gather(rows, own, early, token))
     return gate, up, down, serve_norm.reshape(-1)
 
 

time: 115 us -> 113 us (0.983)
    pallas_call x4, Pallas kernels: 114 us -> 113 us  [the longest x1 76.6 us: first_gather(): pl.pallas_call(functools.partial(first_kernel, model), out_shape=[pltpu.V...]
where the time goes in v3:
time: 113 us
  Pallas kernels  113 us (100%)
    pallas_call x1, Pallas kernels, first_gather(): pl.pallas_call(functools.partial(first_kernel, model), out_shape=[pltpu.V...  76.6 us
    pallas_call x1, Pallas kernels, second_gather(): pl.pallas_call(second_kernel, out_shape=pltpu.VMEM((own.shape[0] * rows,...  26.5 us
    pallas_call x1, Pallas kernels, written(): pl.pallas_call(functools.partial(write_kernel, size), out_shape=[jax.Shap...  6.19 us
    pallas_call x1, Pallas kernels, last_written(): pl.pallas_call(last_kernel, out_shape=jax.ShapeDtypeStruct(down.shape, do...  3.41 us

profile of v3, /device:TPU:0, one launch (start us, length us, event | category | flops | bytes accessed | tf_op | source)
XLA Modules:
  0.0 113.3 jit_solution(10526570679323117599)
XLA Ops:
  0.6 76.6 %shard_map.138 = (bf16[2048,2048]{1,0:T(8,128)(2,1)S(1)}, bf16[2048,2048]{1,0:T(8,128)(2,1)S(1)}, bf16[256,2048]{1,0:T(8,128)(2,1)S(1)}, bf16[3,256,1792]{2,1,0:T(8,128)(2,1)S(1)}, f32[4,4,2,1,128]{4,3,2,1,0:T(1,128)S(1)}) custom-call(bf16[256,2048]{1,0:T(8,128)(2,1)} %refs_0_.1, bf16[64,256]{1,0:T(8,128)(2,1)} %bitcast.7, bf16[64,2048]{1,0:T(8,128)(2,1)} %refs_2_.1, ...), custom_call_target="tpu_custom_call" | custom-call | tf_op jit(solution)/shard_map/pallas_call | solution.py:361
  77.2 6.2 %shard_map.139 = (bf16[2048,2048]{1,0:T(8,128)(2,1)}, bf16[2048,2048]{1,0:T(8,128)(2,1)}, bf16[16,128]{1,0:T(8,128)(2,1)}, f32[8,128]{1,0:T(8,128)S(1)}) custom-call(bf16[2048,2048]{1,0:T(8,128)(2,1)S(1)} %get-tuple-element.13.g, bf16[2048,2048]{1,0:T(8,128)(2,1)S(1)} %get-tuple-element.14.u, f32[4,4,2,1,128]{4,3,2,1,0:T(1,128)S(1)} %get-tuple-element.15.norm), custom_call_target="tpu_custom_call" | custom-call | tf_op jit(solution)/shard_map/pallas_call | solution.py:410
  83.4 26.5 %shard_map.140.d = bf16[2048,2048]{1,0:T(8,128)(2,1)S(1)} custom-call(bf16[256,2048]{1,0:T(8,128)(2,1)S(1)} %get-tuple-element.18.own, bf16[3,256,1792]{2,1,0:T(8,128)(2,1)S(1)} %get-tuple-element.19.early, f32[8,128]{1,0:T(8,128)S(1)} %get-tuple-element.20.token), custom_call_target="tpu_custom_call" | custom-call | tf_op jit(solution)/shard_map/pallas_call | solution.py:380
  109.9 3.4 %shard_map.141 = bf16[2048,2048]{1,0:T(8,128)(2,1)} custom-call(bf16[2048,2048]{1,0:T(8,128)(2,1)S(1)} %shard_map.140.d), custom_call_target="tpu_custom_call" | custom-call | tf_op jit(solution)/shard_map/pallas_call | solution.py:428

commit v4 on v3

--- a/solution.py
+++ b/solution.py
@@ -44,11 +44,19 @@
     )
 
 
+def sent(ref, sem, other):
+    remote(ref, ref, sem, sem, other).wait_send()
+
+
+def came(ref, sem, other):
+    remote(ref, ref, sem, sem, other).wait_recv()
+
+
 def first_kernel(model, *refs):
     sources, (og, ou, own, early, norm), refs = refs[:11], refs[11:16], refs[16:]
     held, refs = refs[:11], refs[11:]
     wg, lg, hg, wu, lu, hu, wd, ld, hd, nt, ns = held
-    fetch_sem, link_send, link_recv, pair_send, pair_recv, early_send, early_recv, norm_send, norm_recv, part = refs
+    fetch_sem, link_send, link_recv, rest_recv, far_recv, pair_send, pair_recv, early_send, early_recv, norm_send, norm_recv, part = refs
     at = Place()
     me, near_x, near_y, far, pair = at.me, at.near_x, at.near_y, at.far, at.pair
     depth = lax.axis_index("model")
@@ -78,19 +86,15 @@
     work = units + [(2, *cut) for cut in cuts((1, 1, 1, 1), wd.shape[0])]
     whole = slice(None)
 
-    for u, (a, start, size) in enumerate(work):
-        if start == 0:
-            fetch(("low", a), 3 * a + 1)
-            if a < 2:
-                fetch(("high", a), 3 * a + 2, whole, pl.ds(0, size))
-            else:
-                fetch(("high", a), 3 * a + 2)
-        if a < 2:
-            fetch(u, 3 * a, whole, pl.ds(start, size))
-        else:
-            fetch(u, 3 * a, pl.ds(start, size), whole)
-        if start == 0 and a < 2:
-            fetch(("rest", a), 3 * a + 2, whole, pl.ds(size, wg.shape[1] - size))
+    first, rest = sum(units[1][1:]), wg.shape[1]
+    fetch("low", 1)
+    fetch("high", 2, whole, pl.ds(0, first))
+    fetch("gate", 0, whole, pl.ds(0, first))
+    fetch("high_rest", 2, whole, pl.ds(first, rest - first))
+    fetch("gate_rest", 0, whole, pl.ds(first, rest - first))
+    for a in (1, 2):
+        for i in (1, 2, 0):
+            fetch((a, i), 3 * a + i)
     fetch("train", 9)
     fetch("step", 10)
     for f in fetches.values():
@@ -102,12 +106,16 @@
 
     def compute(u):
         a, start, size = work[u]
-        if start == 0:
-            fetches["low", a].wait()
-            fetches["high", a].wait()
-        elif a < 2 and work[u - 1][1] == 0:
-            fetches["rest", a].wait()
-        fetches[u].wait()
+        if u == 0:
+            needed = ("low", "high", "gate")
+        elif u == 2:
+            needed = ("high_rest", "gate_rest")
+        elif a and start == 0:
+            needed = [(a, i) for i in range(3)]
+        else:
+            needed = ()
+        for key in needed:
+            fetches[key].wait()
         cut = slice(start, start + size)
         if a < 2:
             w, low, high = ((wg, lg, hg), (wu, lu, hu))[a]
@@ -126,18 +134,28 @@
     def copy(u, owner, send, recv, target):
         return remote(place(u, owner), place(u, owner), send, recv, target)
 
+    far_groups = [list(range(len(UNITS[0]))), list(range(len(UNITS[0]), count - 2)), [count - 2], [count - 1]]
+
     def link(lane, u, owner, target):
-        return copy(u, owner, link_send.at[lane, u], link_recv.at[lane, u], target)
+        if lane == 2:
+            recv = far_recv.at[next(g for g, group in enumerate(far_groups) if u in group)]
+        else:
+            recv = link_recv.at[u] if lane == u % 2 else rest_recv.at[units[u][0]]
+        return copy(u, owner, link_send, recv, target)
 
     def across(lane, u, owner):
-        return copy(u, owner, pair_send.at[lane, u], pair_recv.at[lane, u], pair)
+        return copy(u, owner, pair_send, pair_recv, pair)
+
+    def sized(group):
+        return og.at[pl.ds(0, sum(units[u][2] for u in group)), pl.ds(0, short)]
 
     pieces = cuts(DOWN, own.shape[1])[:EARLY]
 
     def ahead(lane, k, src, target):
         cut = (whole, pl.ds(*pieces[k]))
         src = own.at[cut] if src is None else early.at[(src, *cut)]
-        return remote(src, early.at[(lane, *cut)], early_send.at[lane, k], early_recv.at[lane, k], target)
+        recv = early_recv.at[k if lane == k % 2 else EARLY]
+        return remote(src, early.at[(lane, *cut)], early_send, recv, target)
 
     def send_own(u):
         link(0, u, me, near_x).start()
@@ -160,51 +178,42 @@
     def _():
         norm[chip, depth, 1] = part[...]
 
-    def norm_copy(slot, ref, target):
-        return remote(ref, ref, norm_send.at[slot], norm_recv.at[slot], target)
+    def norm_copy(kind, ref, target):
+        return remote(ref, ref, norm_send.at[kind], norm_recv.at[kind], target)
 
     def norm_part():
-        return remote(part, norm.at[chip, depth, 0], norm_send.at[0], norm_recv.at[0], pair)
-
-    def norm_deep(step, send):
-        return norm_copy(
-            step, norm.at[chip, depth if send else lax.rem(depth + model - step, model)],
-            {"model": lax.rem(depth + step, model)},
-        )
-
-    def norm_wide(lane, owner, target):
-        return norm_copy(model + lane, norm.at[owner // 2], target)
+        return remote(part, norm.at[chip, depth, 0], norm_send.at[4], norm_recv.at[4], pair)
 
     def norm_whole():
-        return norm_copy(model + 3, norm, pair)
+        return norm_copy(3, norm, pair)
 
     def norm_step(u):
         if u == 1:
             norm_part().wait_recv()
             for step in range(1, model):
-                norm_deep(step, True).start()
+                norm_copy(0, norm.at[chip, depth], {"model": lax.rem(depth + step, model)}).start()
         if u == 2:
-            for step in range(1, model):
-                norm_deep(step, False).wait_recv()
-            norm_wide(0, me, near_x).start()
-            norm_wide(1, me, near_y).start()
+            came(norm.at[chip, pl.ds(0, model - 1)], norm_recv.at[0], near_x)
+            norm_copy(1, norm.at[chip], near_x).start()
+            norm_copy(1, norm.at[chip], near_y).start()
         if u == 3:
-            norm_wide(0, near_x, near_x).wait_recv()
-            norm_wide(1, near_y, near_y).wait_recv()
-            norm_wide(2, near_x, near_y).start()
+            came(norm.at[pl.ds(0, 2)], norm_recv.at[1], near_x)
+            norm_copy(2, norm.at[near_x // 2], near_y).start()
         if u == 4:
-            norm_wide(2, far, near_y).wait_recv()
+            came(norm.at[chip], norm_recv.at[2], near_y)
             norm_whole().start()
 
     for u in range(count):
-        link(0, u, near_x, near_x).wait_recv()
-        if u % 2 == 0:
-            link(2, u, near_x, near_y).start()
-        across(0, u, near_x).start()
-        link(1, u, near_y, near_y).wait_recv()
-        if u % 2 == 1:
-            link(2, u, near_y, near_x).start()
-        across(1, u, near_y).start()
+        a, lane = units[u][0], u % 2
+        owner, target = ((near_x, near_y), (near_y, near_x))[lane]
+        link(lane, u, owner, owner).wait_recv()
+        link(2, u, owner, target).start()
+        across(lane, u, owner).start()
+        if u == count - 1 or units[u + 1][0] > a:
+            group = [v for v in range(count) if units[v][0] == a]
+            came(sized(group), rest_recv.at[a], near_x)
+            for v in group:
+                across(1 - v % 2, v, (near_y, near_x)[v % 2]).start()
         if u == 0:
             pl.when(at.core == 0)(lambda: norm_part().start())
         if 1 <= u <= 4:
@@ -216,49 +225,38 @@
             ahead(0, k, None, near_x).start()
             ahead(1, k, None, near_y).start()
 
-    for u in range(count):
-        link(2, u, far, near_x).wait_recv()
-        across(2, u, far).start()
+    for g, group in enumerate(far_groups):
+        came(sized(group), far_recv.at[g], near_x)
+        for u in group:
+            across(2, u, far).start()
 
     @pl.when(at.core == 1)
     def _():
         for k in range(EARLY):
-            ahead(0, k, None, near_x).wait_recv()
-            if k % 2 == 0:
-                ahead(2, k, 0, near_y).start()
-            ahead(1, k, None, near_y).wait_recv()
-            if k % 2 == 1:
-                ahead(2, k, 1, near_x).start()
+            owner, target = ((near_x, near_y), (near_y, near_x))[k % 2]
+            ahead(k % 2, k, None, owner).wait_recv()
+            ahead(2, k, k % 2, target).start()
 
     @pl.when(at.core == 0)
     def _():
         norm_part().wait_send()
         norm_whole().wait_recv()
 
-    for u in range(count):
-        link(0, u, me, near_x).wait_send()
-        link(1, u, me, near_y).wait_send()
-        link(2, u, near_x, near_x).wait_send()
-        for lane, mine, theirs in ((3, me, pair), (0, near_x, at.pair_x), (1, near_y, at.pair_y), (2, far, at.pair_far)):
-            across(lane, u, mine).wait_send()
-            across(lane, u, theirs).wait_recv()
-
-    @pl.when(at.core == 1)
-    def _():
-        for k in range(EARLY):
-            ahead(0, k, None, near_x).wait_send()
-            ahead(1, k, None, near_y).wait_send()
-            ahead(2, k, k % 2, near_x).wait_send()
-            ahead(2, k, None, near_x).wait_recv()
-        for step in range(1, model):
-            norm_deep(step, True).wait_send()
-        norm_wide(0, me, near_x).wait_send()
-        norm_wide(1, me, near_y).wait_send()
-        norm_wide(2, near_x, near_y).wait_send()
-        norm_whole().wait_send()
-
-
-def second_kernel(own, early, token, down, link_send, link_recv, pair_send, pair_recv, ready):
+    @pl.when(at.core == 1)
+    def _():
+        sent(norm.at[chip, pl.ds(0, model - 1)], norm_send.at[0], near_x)
+        sent(norm.at[pl.ds(0, 2)], norm_send.at[1], near_x)
+        sent(norm.at[chip], norm_send.at[2], near_y)
+        sent(norm, norm_send.at[3], pair)
+        sent(early, early_send, near_x)
+        came(early.at[pl.ds(0, 2)], early_recv.at[EARLY], near_x)
+
+    sent(og.at[:, pl.ds(0, 2 * 3 * short)], link_send, near_x)
+    sent(og, pair_send, pair)
+    came(og, pair_recv, pair)
+
+
+def second_kernel(own, early, token, down, link_send, link_recv, rest_recv, far_recv, pair_send, pair_recv, ready):
     at = Place()
     me, near_x, near_y, far, pair = at.me, at.near_x, at.near_y, at.far, at.pair
     short = own.shape[0]
@@ -279,10 +277,11 @@
         return down.at[band(owner), pl.ds(*pieces[k])]
 
     def link(lane, k, src, owner, target):
-        return remote(src, place(k, owner), link_send.at[lane, k], link_recv.at[lane, k], target)
+        recv = far_recv.at[k] if lane == 2 else link_recv.at[k] if lane == k % 2 else rest_recv
+        return remote(src, place(k, owner), link_send, recv, target)
 
     def across(lane, k, src, owner):
-        return remote(src, place(k, owner), pair_send.at[lane, k], pair_recv.at[lane, k], pair)
+        return remote(src, place(k, owner), pair_send, pair_recv, pair)
 
     def gather(first):
         late, everything = range(first, len(pieces)), range(len(pieces))
@@ -304,16 +303,15 @@
             end = sum(pieces[first - 1])
             for lane, owner in enumerate((near_x, near_y, far)):
                 down[band(owner), :end] = early[lane]
+        width = own.shape[1] - pieces[first][0]
         for k in late:
-            link(0, k, place(k, near_x), near_x, near_x).wait_recv()
-            if k % 2 == 0:
-                link(2, k, place(k, near_x), near_x, near_y).start()
-            link(1, k, place(k, near_y), near_y, near_y).wait_recv()
-            if k % 2 == 1:
-                link(2, k, place(k, near_y), near_y, near_x).start()
+            owner, target = ((near_x, near_y), (near_y, near_x))[k % 2]
+            link(k % 2, k, place(k, owner), owner, owner).wait_recv()
+            link(2, k, place(k, owner), owner, target).start()
         if not first:
             pl.semaphore_wait(ready, 1)
             over()
+        came(down.at[pl.ds(0, short), pl.ds(0, width)], rest_recv, near_x)
         for k in late:
             across(0, k, place(k, near_x), near_x).start()
             across(1, k, place(k, near_y), near_y).start()
@@ -321,14 +319,9 @@
             link(2, k, place(k, far), far, near_x).wait_recv()
             across(2, k, place(k, far), far).start()
 
-        for k in late:
-            link(0, k, own.at[cut(k)], me, near_x).wait_send()
-            link(1, k, own.at[cut(k)], me, near_y).wait_send()
-            link(2, k, place(k, near_x), near_x, near_x).wait_send()
-        for k in everything:
-            for lane, mine, theirs in ((3, me, pair), (0, near_x, at.pair_x), (1, near_y, at.pair_y), (2, far, at.pair_far)):
-                across(lane, k, place(k, mine), mine).wait_send()
-                across(lane, k, place(k, theirs), theirs).wait_recv()
+        sent(down.at[pl.ds(0, 3 * short), pl.ds(0, width)], link_send, near_x)
+        sent(down.at[pl.ds(0, 4 * short), :], pair_send, pair)
+        came(down.at[pl.ds(0, 4 * short), :], pair_recv, pair)
 
     @pl.when(at.core == 0)
     def _():
@@ -365,9 +358,9 @@
         out_specs=[VMEM] * 5,
         scratch_shapes=[pltpu.VMEM(a.shape, a.dtype) for a in arrays]
         + [
-            dma((count + 14,)),
-            dma((3, count)), dma((3, count)), dma((4, count)), dma((4, count)),
-            dma((3, EARLY)), dma((3, EARLY)), dma((model + 4,)), dma((model + 4,)),
+            dma((13,)),
+            dma(()), dma((count,)), dma((2,)), dma((4,)), dma(()), dma(()),
+            dma(()), dma((EARLY + 1,)), dma((5,)), dma((5,)),
             pltpu.VMEM((1, lanes), jnp.float32),
         ],
         compiler_params=pltpu.CompilerParams(collective_id=0, has_side_effects=True, vmem_limit_bytes=44 * MIB),
@@ -383,7 +376,7 @@
         in_specs=[VMEM, VMEM, HBM],
         out_specs=VMEM,
         scratch_shapes=[
-            dma((3, count)), dma((3, count)), dma((4, count)), dma((4, count)), pltpu.SemaphoreType.REGULAR,
+            dma(()), dma((count,)), dma(()), dma((count,)), dma(()), dma(()), pltpu.SemaphoreType.REGULAR,
         ],
         compiler_params=pltpu.CompilerParams(collective_id=1, has_side_effects=True, vmem_limit_bytes=4 * MIB),
     )(own, early, token)

time: 113 us -> 113 us (level)
  no operation moved by 1% of the time
where the time goes in v4:
time: 113 us
  Pallas kernels  112 us (99%)
    pallas_call x1, Pallas kernels, first_gather(): pl.pallas_call(functools.partial(first_kernel, model), out_shape=[pltpu.V...  75.6 us
    pallas_call x1, Pallas kernels, second_gather(): pl.pallas_call(second_kernel, out_shape=pltpu.VMEM((own.shape[0] * rows,...  26.9 us
    pallas_call x1, Pallas kernels, written(): pl.pallas_call(functools.partial(write_kernel, size), out_shape=[jax.Shap...  6.19 us
    pallas_call x1, Pallas kernels, last_written(): pl.pallas_call(last_kernel, out_shape=jax.ShapeDtypeStruct(down.shape, do...  3.41 us

profile of v4, /device:TPU:0, one launch (start us, length us, event | category | flops | bytes accessed | tf_op | source)
XLA Modules:
  0.0 112.7 jit_solution(2201419924796687497)
XLA Ops:
  0.6 75.6 %shard_map.138 = (bf16[2048,2048]{1,0:T(8,128)(2,1)S(1)}, bf16[2048,2048]{1,0:T(8,128)(2,1)S(1)}, bf16[256,2048]{1,0:T(8,128)(2,1)S(1)}, bf16[3,256,1792]{2,1,0:T(8,128)(2,1)S(1)}, f32[4,4,2,1,128]{4,3,2,1,0:T(1,128)S(1)}) custom-call(bf16[256,2048]{1,0:T(8,128)(2,1)} %refs_0_.1, bf16[64,256]{1,0:T(8,128)(2,1)} %bitcast.7, bf16[64,2048]{1,0:T(8,128)(2,1)} %refs_2_.1, ...), custom_call_target="tpu_custom_call" | custom-call | tf_op jit(solution)/shard_map/pallas_call | solution.py:354
  76.2 6.2 %shard_map.139 = (bf16[2048,2048]{1,0:T(8,128)(2,1)}, bf16[2048,2048]{1,0:T(8,128)(2,1)}, bf16[16,128]{1,0:T(8,128)(2,1)}, f32[8,128]{1,0:T(8,128)S(1)}) custom-call(bf16[2048,2048]{1,0:T(8,128)(2,1)S(1)} %get-tuple-element.13.g, bf16[2048,2048]{1,0:T(8,128)(2,1)S(1)} %get-tuple-element.14.u, f32[4,4,2,1,128]{4,3,2,1,0:T(1,128)S(1)} %get-tuple-element.15.norm), custom_call_target="tpu_custom_call" | custom-call | tf_op jit(solution)/shard_map/pallas_call | solution.py:403
  82.4 26.9 %shard_map.140.d = bf16[2048,2048]{1,0:T(8,128)(2,1)S(1)} custom-call(bf16[256,2048]{1,0:T(8,128)(2,1)S(1)} %get-tuple-element.18.own, bf16[3,256,1792]{2,1,0:T(8,128)(2,1)S(1)} %get-tuple-element.19.early, f32[8,128]{1,0:T(8,128)S(1)} %get-tuple-element.20.token), custom_call_target="tpu_custom_call" | custom-call | tf_op jit(solution)/shard_map/pallas_call | solution.py:373
  109.3 3.4 %shard_map.141 = bf16[2048,2048]{1,0:T(8,128)(2,1)} custom-call(bf16[2048,2048]{1,0:T(8,128)(2,1)S(1)} %shard_map.140.d), custom_call_target="tpu_custom_call" | custom-call | tf_op jit(solution)/shard_map/pallas_call | solution.py:421

commit v5 on v4

--- a/solution.py
+++ b/solution.py
@@ -9,8 +9,8 @@
 
 mix_rate = 0.5
 MESH = pl.DeviceIdType.MESH
-UNITS = ((1, 1, 3, 3, 4, 4), (4, 4, 3, 3, 1, 1))
-DOWN = (4, 4, 3, 3, 1, 1)
+UNITS = ((2, 2, 2, 2, 4, 4), (4, 4, 4, 4), (1, 1))
+DOWN = (4, 4, 2, 2, 1, 1)
 EARLY = 4
 SIDE = 2
 
@@ -18,6 +18,13 @@
 def cuts(parts, size):
     whole = sum(parts)
     return [(sum(parts[:i]) * size // whole, parts[i] * size // whole) for i in range(len(parts))]
+
+
+def down_cuts(size):
+    pieces = cuts(UNITS[2] + DOWN, size)
+    head = len(UNITS[2])
+    offset = pieces[head][0]
+    return pieces[:head], [(start - offset, length) for start, length in pieces[head:]]
 
 
 class Place:
@@ -53,7 +60,7 @@
 
 
 def first_kernel(model, *refs):
-    sources, (og, ou, own, early, norm), refs = refs[:11], refs[11:16], refs[16:]
+    sources, (og, ou, od, own, early, norm), refs = refs[:11], refs[11:17], refs[17:]
     held, refs = refs[:11], refs[11:]
     wg, lg, hg, wu, lu, hu, wd, ld, hd, nt, ns = held
     fetch_sem, link_send, link_recv, rest_recv, far_recv, pair_send, pair_recv, early_send, early_recv, norm_send, norm_recv, part = refs
@@ -62,16 +69,7 @@
     depth = lax.axis_index("model")
     chip = me // 2
 
-    barrier = pltpu.get_barrier_semaphore()
-    for other in (near_x, near_y, pair):
-        pl.semaphore_signal(barrier, inc=1, device_id={"rows": other}, device_id_type=MESH)
-
-    @pl.when(at.core == 1)
-    def _():
-        for step in range(1, model):
-            pl.semaphore_signal(barrier, inc=1, device_id={"model": lax.rem(depth + step, model)}, device_id_type=MESH)
-
-    outs = (og, ou)
+    outs = (og, ou, od)
     fetches = {}
 
     def fetch(key, i, *cut):
@@ -81,9 +79,11 @@
         )
 
     short, short_down = wg.shape[0], wd.shape[1]
-    units = [(a, *cut) for a in range(2) for cut in cuts(UNITS[a], wg.shape[1])]
+    heads, pieces = down_cuts(wd.shape[0])
+    offset = sum(heads[-1])
+    units = [(a, *cut) for a in range(2) for cut in cuts(UNITS[a], wg.shape[1])] + [(2, *cut) for cut in heads]
     count = len(units)
-    work = units + [(2, *cut) for cut in cuts((1, 1, 1, 1), wd.shape[0])]
+    work = units + [(2, offset + start, size) for start, size in pieces]
     whole = slice(None)
 
     first, rest = sum(units[1][1:]), wg.shape[1]
@@ -97,11 +97,23 @@
             fetch((a, i), 3 * a + i)
     fetch("train", 9)
     fetch("step", 10)
-    for f in fetches.values():
-        f.start()
+    urgent = ("low", "high", "gate")
+    for key in urgent:
+        fetches[key].start()
+
+    barrier = pltpu.get_barrier_semaphore()
+    for other in (near_x, near_y, pair):
+        pl.semaphore_signal(barrier, inc=1, device_id={"rows": other}, device_id_type=MESH)
+
+    @pl.when(at.core == 1)
+    def _():
+        for step in range(1, model):
+            pl.semaphore_signal(barrier, inc=1, device_id={"model": lax.rem(depth + step, model)}, device_id_type=MESH)
 
     def place(u, owner):
         a, start, size = units[u]
+        if a == 2:
+            return od.at[pl.ds(pl.multiple_of(owner * short_down, short_down), short_down), pl.ds(start, size)]
         return outs[a].at[pl.ds(start, size), pl.ds(pl.multiple_of(owner * short, short), short)]
 
     def compute(u):
@@ -110,7 +122,7 @@
             needed = ("low", "high", "gate")
         elif u == 2:
             needed = ("high_rest", "gate_rest")
-        elif a and start == 0:
+        elif a and work[u - 1][0] < a:
             needed = [(a, i) for i in range(3)]
         else:
             needed = ()
@@ -126,10 +138,10 @@
             low, high, (((0,), (0,)), ((), ())), preferred_element_type=jnp.float32
         )
         merged = merged.astype(jnp.bfloat16).T
-        if a < 2:
+        if u < count:
             place(u, me)[...] = merged
         else:
-            own[:, cut] = merged
+            own[:, start - offset : start - offset + size] = merged
 
     def copy(u, owner, send, recv, target):
         return remote(place(u, owner), place(u, owner), send, recv, target)
@@ -141,15 +153,13 @@
             recv = far_recv.at[next(g for g, group in enumerate(far_groups) if u in group)]
         else:
             recv = link_recv.at[u] if lane == u % 2 else rest_recv.at[units[u][0]]
-        return copy(u, owner, link_send, recv, target)
+        return copy(u, owner, link_send.at[units[u][0] // 2], recv, target)
 
     def across(lane, u, owner):
-        return copy(u, owner, pair_send, pair_recv, pair)
+        return copy(u, owner, pair_send.at[units[u][0] // 2], pair_recv.at[units[u][0] // 2], pair)
 
     def sized(group):
         return og.at[pl.ds(0, sum(units[u][2] for u in group)), pl.ds(0, short)]
-
-    pieces = cuts(DOWN, own.shape[1])[:EARLY]
 
     def ahead(lane, k, src, target):
         cut = (whole, pl.ds(*pieces[k]))
@@ -163,6 +173,9 @@
         across(3, u, me).start()
 
     compute(0)
+    for key, f in fetches.items():
+        if key not in urgent:
+            f.start()
     pl.semaphore_wait(barrier, 3 + at.core * (model - 1))
     for u in range(1, count + 1):
         compute(u)
@@ -251,9 +264,12 @@
         sent(early, early_send, near_x)
         came(early.at[pl.ds(0, 2)], early_recv.at[EARLY], near_x)
 
-    sent(og.at[:, pl.ds(0, 2 * 3 * short)], link_send, near_x)
-    sent(og, pair_send, pair)
-    came(og, pair_recv, pair)
+    sent(og.at[:, pl.ds(0, 2 * 3 * short)], link_send.at[0], near_x)
+    sent(od.at[pl.ds(0, 3 * short_down)], link_send.at[1], near_x)
+    sent(og, pair_send.at[0], pair)
+    sent(od.at[pl.ds(0, 4 * short_down)], pair_send.at[1], pair)
+    came(og, pair_recv.at[0], pair)
+    came(od.at[pl.ds(0, 4 * short_down)], pair_recv.at[1], pair)
 
 
 def second_kernel(own, early, token, down, link_send, link_recv, rest_recv, far_recv, pair_send, pair_recv, ready):
@@ -337,33 +353,36 @@
 HBM = pl.BlockSpec(memory_space=pltpu.HBM)
 VMEM = pl.BlockSpec(memory_space=pltpu.VMEM)
 MIB = 2**20
+GRANT = 42
 
 
 def first_gather(rows, model, arrays):
     weight_gate, weight_up, weight_down, norm_train = arrays[0], arrays[3], arrays[6], arrays[9]
-    own = (weight_down.shape[1], weight_down.shape[0])
+    heads, pieces = down_cuts(weight_down.shape[0])
+    short, head = weight_down.shape[1], sum(heads[-1])
     shapes = [
         (weight_gate.shape[1], weight_gate.shape[0] * rows),
         (weight_up.shape[1], weight_up.shape[0] * rows),
-        own,
-        (3, own[0], sum(cuts(DOWN, own[1])[EARLY - 1])),
+        (short * rows, head),
+        (short, weight_down.shape[0] - head),
+        (3, short, sum(pieces[EARLY - 1])),
     ]
     lanes = -(-norm_train.shape[1] // 128) * 128
-    count = len(UNITS[0]) + len(UNITS[1])
+    count = sum(len(parts) for parts in UNITS)
     dma = pltpu.SemaphoreType.DMA
     return pl.pallas_call(
         functools.partial(first_kernel, model),
         out_shape=[pltpu.VMEM(s, jnp.bfloat16) for s in shapes] + [pltpu.VMEM((rows // 2, model, 2, 1, lanes), jnp.float32)],
         in_specs=[HBM] * len(arrays),
-        out_specs=[VMEM] * 5,
+        out_specs=[VMEM] * 6,
         scratch_shapes=[pltpu.VMEM(a.shape, a.dtype) for a in arrays]
         + [
             dma((13,)),
-            dma(()), dma((count,)), dma((2,)), dma((4,)), dma(()), dma(()),
+            dma((2,)), dma((count,)), dma((3,)), dma((4,)), dma((2,)), dma((2,)),
             dma(()), dma((EARLY + 1,)), dma((5,)), dma((5,)),
             pltpu.VMEM((1, lanes), jnp.float32),
         ],
-        compiler_params=pltpu.CompilerParams(collective_id=0, has_side_effects=True, vmem_limit_bytes=44 * MIB),
+        compiler_params=pltpu.CompilerParams(collective_id=0, has_side_effects=True, vmem_limit_bytes=GRANT * MIB),
     )(*arrays)
 
 
@@ -382,59 +401,62 @@
     )(own, early, token)
 
 
-def write_kernel(size, g, u, norm, og, ou, out, token, packed_norm, sems):
-    copies = [pltpu.make_async_copy(s, t, sems.at[i]) for i, (s, t) in enumerate(((g, og), (u, ou), (packed_norm, out)))]
-    copies[0].start()
-    copies[1].start()
+def write_kernel(size, g, u, d, norm, og, ou, od, out, token, packed_norm, sems):
+    pairs = ((g, og), (u, ou), (d, od.at[:, pl.ds(0, d.shape[1])]), (packed_norm, out))
+    copies = [pltpu.make_async_copy(s, t, sems.at[i]) for i, (s, t) in enumerate(pairs)]
+    for c in copies[:3]:
+        c.start()
     token[...] = jnp.zeros(token.shape, token.dtype)
     chips, model, cores, _, lanes = norm.shape
     parts = [norm[r, m, c][:, :size] for r in range(chips) for c in range(cores) for m in range(model)]
     group = lanes // size
     packed = [jnp.concatenate(parts[i : i + group], axis=1) for i in range(0, len(parts), group)]
     packed_norm[...] = jnp.concatenate(packed, axis=0).astype(out.dtype)
-    copies[2].start()
+    copies[3].start()
     for c in copies:
         c.wait()
 
 
-def written(size, gate, up, norm):
+def written(size, gate, up, down, width, norm):
     chips, model, cores, _, lanes = norm.shape
     packed = (chips * model * cores * size // lanes, lanes)
     return pl.pallas_call(
         functools.partial(write_kernel, size),
-        out_shape=[jax.ShapeDtypeStruct(s, jnp.bfloat16) for s in (gate.shape, up.shape, packed)]
+        out_shape=[jax.ShapeDtypeStruct(s, jnp.bfloat16) for s in (gate.shape, up.shape, (down.shape[0], width), packed)]
         + [jax.ShapeDtypeStruct((8, 128), jnp.float32)],
-        in_specs=[VMEM] * 3,
-        out_specs=[HBM] * 3 + [VMEM],
-        scratch_shapes=[pltpu.VMEM(packed, jnp.bfloat16), pltpu.SemaphoreType.DMA((3,))],
+        in_specs=[VMEM] * 4,
+        out_specs=[HBM] * 4 + [VMEM],
+        scratch_shapes=[pltpu.VMEM(packed, jnp.bfloat16), pltpu.SemaphoreType.DMA((4,))],
         compiler_params=pltpu.CompilerParams(vmem_limit_bytes=MIB),
-    )(gate, up, norm)
-
-
-def last_kernel(d, od, sem):
-    c = pltpu.make_async_copy(d, od, sem)
+    )(gate, up, down, norm)
+
+
+def last_kernel(d, begun, od, sem):
+    width = d.shape[1]
+    c = pltpu.make_async_copy(d, od.at[:, pl.ds(od.shape[1] - width, width)], sem)
     c.start()
     c.wait()
 
 
-def last_written(down):
+def last_written(down, begun):
     return pl.pallas_call(
         last_kernel,
-        out_shape=jax.ShapeDtypeStruct(down.shape, down.dtype),
-        in_specs=[VMEM],
+        out_shape=jax.ShapeDtypeStruct(begun.shape, begun.dtype),
+        in_specs=[VMEM, HBM],
         out_specs=HBM,
+        input_output_aliases={1: 0},
         scratch_shapes=[pltpu.SemaphoreType.DMA(())],
         compiler_params=pltpu.CompilerParams(vmem_limit_bytes=MIB),
-    )(down)
+    )(down, begun)
 
 
 def local_kernel(rows, model, *arrays):
     arrays = tuple(a.T if i in (1, 4, 7) else a for i, a in enumerate(arrays[:9])) + tuple(
         a.reshape(1, -1) for a in arrays[9:]
     )
-    gate, up, own, early, norm = first_gather(rows, model, arrays)
-    gate, up, serve_norm, token = written(arrays[9].shape[1], gate, up, norm)
-    down = last_written(second_gather(rows, own, early, token))
+    gate, up, down, own, early, norm = first_gather(rows, model, arrays)
+    gate, up, down, serve_norm, token = written(arrays[9].shape[1], gate, up, down, arrays[6].shape[0], norm)
+    down = last_written(second_gather(rows, own, early, token), down)
     return gate, up, down, serve_norm.reshape(-1)
 
 

time: 113 us -> 113 us (level)
    pallas_call x1, Pallas kernels: 26.9 us -> 22.4 us  [second_gather(): pl.pallas_call(second_kernel, out_shape=pltpu.VMEM((own.shape[0] * rows,...]
    pallas_call x1, Pallas kernels: 75.6 us -> 80 us  [first_gather(): pl.pallas_call(functools.partial(first_kernel, model), out_shape=[pltpu.V...]
where the time goes in v5:
time: 113 us; the launch traced here: 112 us
  Pallas kernels  112 us (99%)
    pallas_call x1, Pallas kernels, first_gather(): pl.pallas_call(functools.partial(first_kernel, model), out_shape=[pltpu.V...  80 us
    pallas_call x1, Pallas kernels, second_gather(): pl.pallas_call(second_kernel, out_shape=pltpu.VMEM((own.shape[0] * rows,...  22.4 us
    pallas_call x1, Pallas kernels, written(): pl.pallas_call(functools.partial(write_kernel, size), out_shape=[jax.Shap...  6.29 us
    pallas_call x1, Pallas kernels, last_written(): pl.pallas_call(last_kernel, out_shape=jax.ShapeDtypeStruct(begun.shape, b...  3.06 us

profile of v5, /device:TPU:0, one launch (start us, length us, event | category | flops | bytes accessed | tf_op | source)
XLA Modules:
  0.0 112.4 jit_solution(13917846782122826692)
XLA Ops:
  0.6 80.0 %shard_map.138 = (bf16[2048,2048]{1,0:T(8,128)(2,1)S(1)}, bf16[2048,2048]{1,0:T(8,128)(2,1)S(1)}, bf16[2048,256]{1,0:T(8,128)(2,1)S(1)}, bf16[256,1792]{1,0:T(8,...) custom-call(bf16[256,2048]{1,0:T(8,128)(2,1)} %refs_0_.1, bf16[64,256]{1,0:T(8,128)(2,1)} %bitcast.7, ...), custom_call_target="tpu_custom_call" | custom-call | tf_op jit(solution)/shard_map/pallas_call | solution.py:373
  80.7 6.3 %shard_map.139 = (bf16[2048,2048]{1,0:T(8,128)(2,1)}, bf16[2048,2048]{1,0:T(8,128)(2,1)}, bf16[2048,2048]{1,0:T(8,128)(2,1)}, bf16[16,128]{1,0:T(8,128)(2,1)}, f32[8,128]{1,0:T(8,128)S(1)}) custom-call(bf16[2048,2048]{1,0:T(8,128)(2,1)S(1)} %get-tuple-element.15.g, bf16[2048,2048]{1,0:T(8,128)(2,1)S(1)} %get-tuple-element.16.u, ...), custom_call_target="tpu_custom_call" | custom-call | tf_op jit(solution)/shard_map/pallas_call | solution.py:423
  87.0 22.4 %shard_map.140.d = bf16[2048,1792]{1,0:T(8,128)(2,1)S(1)} custom-call(bf16[256,1792]{1,0:T(8,128)(2,1)S(1)} %get-tuple-element.21.own, bf16[3,256,1536]{2,1,0:T(8,128)(2,1)S(1)} %get-tuple-element.22.early, f32[8,128]{1,0:T(8,128)S(1)} %get-tuple-element.23.token), custom_call_target="tpu_custom_call" | custom-call | tf_op jit(solution)/shard_map/pallas_call | solution.py:392
  109.4 3.1 %shard_map.141 = bf16[2048,2048]{1,0:T(8,128)(2,1)} custom-call(bf16[2048,1792]{1,0:T(8,128)(2,1)S(1)} %shard_map.140.d, bf16[2048,2048]{1,0:T(8,128)(2,1)} %get-tuple-element.24.begun), custom_call_target="tpu_custom_call", output_to_operand_aliasing={{}: (1, {})} | custom-call | tf_op jit(solution)/shard_map/pallas_call | solution.py:442

commit v6 on v5

--- a/solution.py
+++ b/solution.py
@@ -314,7 +314,6 @@
 
         if first:
             over()
-        down[band(me), :] = own[...]
         if first:
             end = sum(pieces[first - 1])
             for lane, owner in enumerate((near_x, near_y, far)):
@@ -401,10 +400,15 @@
     )(own, early, token)
 
 
-def write_kernel(size, g, u, d, norm, og, ou, od, out, token, packed_norm, sems):
-    pairs = ((g, og), (u, ou), (d, od.at[:, pl.ds(0, d.shape[1])]), (packed_norm, out))
+def write_kernel(size, g, u, d, own, norm, og, ou, od, out, token, packed_norm, sems):
+    short = own.shape[0]
+    mine = pl.ds(pl.multiple_of(lax.axis_index("rows") * short, short), short)
+    pairs = (
+        (g, og), (u, ou), (d, od.at[:, pl.ds(0, d.shape[1])]), (own, od.at[mine, pl.ds(d.shape[1], own.shape[1])]),
+        (packed_norm, out),
+    )
     copies = [pltpu.make_async_copy(s, t, sems.at[i]) for i, (s, t) in enumerate(pairs)]
-    for c in copies[:3]:
+    for c in copies[:4]:
         c.start()
     token[...] = jnp.zeros(token.shape, token.dtype)
     chips, model, cores, _, lanes = norm.shape
@@ -412,40 +416,47 @@
     group = lanes // size
     packed = [jnp.concatenate(parts[i : i + group], axis=1) for i in range(0, len(parts), group)]
     packed_norm[...] = jnp.concatenate(packed, axis=0).astype(out.dtype)
-    copies[3].start()
+    copies[4].start()
     for c in copies:
         c.wait()
 
 
-def written(size, gate, up, down, width, norm):
+def written(size, gate, up, down, width, own, norm):
     chips, model, cores, _, lanes = norm.shape
     packed = (chips * model * cores * size // lanes, lanes)
     return pl.pallas_call(
         functools.partial(write_kernel, size),
         out_shape=[jax.ShapeDtypeStruct(s, jnp.bfloat16) for s in (gate.shape, up.shape, (down.shape[0], width), packed)]
         + [jax.ShapeDtypeStruct((8, 128), jnp.float32)],
-        in_specs=[VMEM] * 4,
+        in_specs=[VMEM] * 5,
         out_specs=[HBM] * 4 + [VMEM],
-        scratch_shapes=[pltpu.VMEM(packed, jnp.bfloat16), pltpu.SemaphoreType.DMA((4,))],
+        scratch_shapes=[pltpu.VMEM(packed, jnp.bfloat16), pltpu.SemaphoreType.DMA((5,))],
         compiler_params=pltpu.CompilerParams(vmem_limit_bytes=MIB),
-    )(gate, up, down, norm)
-
-
-def last_kernel(d, begun, od, sem):
-    width = d.shape[1]
-    c = pltpu.make_async_copy(d, od.at[:, pl.ds(od.shape[1] - width, width)], sem)
-    c.start()
-    c.wait()
-
-
-def last_written(down, begun):
+    )(gate, up, down, own, norm)
+
+
+def last_kernel(rows, d, begun, od, sems):
+    me, width, short = lax.axis_index("rows"), d.shape[1], d.shape[0] // rows
+    copies = []
+    for step in range(1, rows):
+        band = pl.ds(pl.multiple_of(lax.rem(me + step, rows) * short, short), short)
+        copies.append(
+            pltpu.make_async_copy(d.at[band], od.at[band, pl.ds(od.shape[1] - width, width)], sems.at[step - 1])
+        )
+    for c in copies:
+        c.start()
+    for c in copies:
+        c.wait()
+
+
+def last_written(rows, down, begun):
     return pl.pallas_call(
-        last_kernel,
+        functools.partial(last_kernel, rows),
         out_shape=jax.ShapeDtypeStruct(begun.shape, begun.dtype),
         in_specs=[VMEM, HBM],
         out_specs=HBM,
         input_output_aliases={1: 0},
-        scratch_shapes=[pltpu.SemaphoreType.DMA(())],
+        scratch_shapes=[pltpu.SemaphoreType.DMA((rows - 1,))],
         compiler_params=pltpu.CompilerParams(vmem_limit_bytes=MIB),
     )(down, begun)
 
@@ -455,8 +466,8 @@
         a.reshape(1, -1) for a in arrays[9:]
     )
     gate, up, down, own, early, norm = first_gather(rows, model, arrays)
-    gate, up, down, serve_norm, token = written(arrays[9].shape[1], gate, up, down, arrays[6].shape[0], norm)
-    down = last_written(second_gather(rows, own, early, token), down)
+    gate, up, down, serve_norm, token = written(arrays[9].shape[1], gate, up, down, arrays[6].shape[0], own, norm)
+    down = last_written(rows, second_gather(rows, own, early, token), down)
     return gate, up, down, serve_norm.reshape(-1)
 
 

time: 113 us -> 112 us (level)
  no operation moved by 1% of the time
where the time goes in v6:
time: 112 us
  Pallas kernels  111 us (99%)
    pallas_call x1, Pallas kernels, first_gather(): pl.pallas_call(functools.partial(first_kernel, model), out_shape=[pltpu.V...  80 us
    pallas_call x1, Pallas kernels, second_gather(): pl.pallas_call(second_kernel, out_shape=pltpu.VMEM((own.shape[0] * rows,...  22.1 us
    pallas_call x1, Pallas kernels, written(): pl.pallas_call(functools.partial(write_kernel, size), out_shape=[jax.Shap...  6.57 us
    pallas_call x1, Pallas kernels, last_written(): pl.pallas_call(functools.partial(last_kernel, rows), out_shape=jax.ShapeD...  2.79 us

profile of v6, /device:TPU:0, one launch (start us, length us, event | category | flops | bytes accessed | tf_op | source)
XLA Modules:
  0.0 112.2 jit_solution(13840463403429212543)
XLA Ops:
  0.6 80.0 %shard_map.138 = (bf16[2048,2048]{1,0:T(8,128)(2,1)S(1)}, bf16[2048,2048]{1,0:T(8,128)(2,1)S(1)}, bf16[2048,256]{1,0:T(8,128)(2,1)S(1)}, bf16[256,1792]{1,0:T(8,...) custom-call(bf16[256,2048]{1,0:T(8,128)(2,1)} %refs_0_.1, bf16[64,256]{1,0:T(8,128)(2,1)} %bitcast.7, ...), custom_call_target="tpu_custom_call" | custom-call | tf_op jit(solution)/shard_map/pallas_call | solution.py:372
  80.7 6.6 %shard_map.139 = (bf16[2048,2048]{1,0:T(8,128)(2,1)}, bf16[2048,2048]{1,0:T(8,128)(2,1)}, bf16[2048,2048]{1,0:T(8,128)(2,1)}, bf16[16,128]{1,0:T(8,128)(2,1)}, f32[8,128]{1,0:T(8,128)S(1)}) custom-call(bf16[2048,2048]{1,0:T(8,128)(2,1)S(1)} %get-tuple-element.15.g, bf16[2048,2048]{1,0:T(8,128)(2,1)S(1)} %get-tuple-element.16.u, ...), custom_call_target="tpu_custom_call" | custom-call | tf_op jit(solution)/shard_map/pallas_call | solution.py:427
  87.2 22.1 %shard_map.140.d = bf16[2048,1792]{1,0:T(8,128)(2,1)S(1)} custom-call(bf16[256,1792]{1,0:T(8,128)(2,1)S(1)} %get-tuple-element.18.own, bf16[3,256,1536]{2,1,0:T(8,128)(2,1)S(1)} %get-tuple-element.22.early, f32[8,128]{1,0:T(8,128)S(1)} %get-tuple-element.23.token), custom_call_target="tpu_custom_call" | custom-call | tf_op jit(solution)/shard_map/pallas_call | solution.py:391
  109.4 2.8 %shard_map.141 = bf16[2048,2048]{1,0:T(8,128)(2,1)} custom-call(bf16[2048,1792]{1,0:T(8,128)(2,1)S(1)} %shard_map.140.d, bf16[2048,2048]{1,0:T(8,128)(2,1)} %get-tuple-element.24.begun), custom_call_target="tpu_custom_call", output_to_operand_aliasing={{}: (1, {})} | custom-call | tf_op jit(solution)/shard_map/pallas_call | solution.py:453

commit v7 on v6

--- a/solution.py
+++ b/solution.py
@@ -9,7 +9,7 @@
 
 mix_rate = 0.5
 MESH = pl.DeviceIdType.MESH
-UNITS = ((2, 2, 2, 2, 4, 4), (4, 4, 4, 4), (1, 1))
+UNITS = ((1, 1, 6, 6, 1, 1), (7, 7, 1, 1), (1, 1))
 DOWN = (4, 4, 2, 2, 1, 1)
 EARLY = 4
 SIDE = 2

time: 112 us -> 112 us (level)
  no operation moved by 1% of the time
where the time goes in v7:
time: 112 us
  Pallas kernels  112 us (100%)
    pallas_call x1, Pallas kernels, first_gather(): pl.pallas_call(functools.partial(first_kernel, model), out_shape=[pltpu.V...  80.2 us
    pallas_call x1, Pallas kernels, second_gather(): pl.pallas_call(second_kernel, out_shape=pltpu.VMEM((own.shape[0] * rows,...  22.1 us
    pallas_call x1, Pallas kernels, written(): pl.pallas_call(functools.partial(write_kernel, size), out_shape=[jax.Shap...  6.57 us
    pallas_call x1, Pallas kernels, last_written(): pl.pallas_call(functools.partial(last_kernel, rows), out_shape=jax.ShapeD...  2.79 us

profile of v7, /device:TPU:0, one launch (start us, length us, event | category | flops | bytes accessed | tf_op | source)
XLA Modules:
  0.0 112.3 jit_solution(2330680120099947068)
XLA Ops:
  0.6 80.2 %shard_map.138 = (bf16[2048,2048]{1,0:T(8,128)(2,1)S(1)}, bf16[2048,2048]{1,0:T(8,128)(2,1)S(1)}, bf16[2048,256]{1,0:T(8,128)(2,1)S(1)}, bf16[256,1792]{1,0:T(8,...) custom-call(bf16[256,2048]{1,0:T(8,128)(2,1)} %refs_0_.1, bf16[64,256]{1,0:T(8,128)(2,1)} %bitcast.7, ...), custom_call_target="tpu_custom_call" | custom-call | tf_op jit(solution)/shard_map/pallas_call | solution.py:372
  80.9 6.6 %shard_map.139 = (bf16[2048,2048]{1,0:T(8,128)(2,1)}, bf16[2048,2048]{1,0:T(8,128)(2,1)}, bf16[2048,2048]{1,0:T(8,128)(2,1)}, bf16[16,128]{1,0:T(8,128)(2,1)}, f32[8,128]{1,0:T(8,128)S(1)}) custom-call(bf16[2048,2048]{1,0:T(8,128)(2,1)S(1)} %get-tuple-element.15.g, bf16[2048,2048]{1,0:T(8,128)(2,1)S(1)} %get-tuple-element.16.u, ...), custom_call_target="tpu_custom_call" | custom-call | tf_op jit(solution)/shard_map/pallas_call | solution.py:427
  87.4 22.1 %shard_map.140.d = bf16[2048,1792]{1,0:T(8,128)(2,1)S(1)} custom-call(bf16[256,1792]{1,0:T(8,128)(2,1)S(1)} %get-tuple-element.18.own, bf16[3,256,1536]{2,1,0:T(8,128)(2,1)S(1)} %get-tuple-element.22.early, f32[8,128]{1,0:T(8,128)S(1)} %get-tuple-element.23.token), custom_call_target="tpu_custom_call" | custom-call | tf_op jit(solution)/shard_map/pallas_call | solution.py:391
  109.6 2.8 %shard_map.141 = bf16[2048,2048]{1,0:T(8,128)(2,1)} custom-call(bf16[2048,1792]{1,0:T(8,128)(2,1)S(1)} %shard_map.140.d, bf16[2048,2048]{1,0:T(8,128)(2,1)} %get-tuple-element.24.begun), custom_call_target="tpu_custom_call", output_to_operand_aliasing={{}: (1, {})} | custom-call | tf_op jit(solution)/shard_map/pallas_call | solution.py:453
